TPU v7x, 32 devices: a whole 2x2x4 slice. The times are simulated.
32 devices in a mesh: dp: 2 (over x), cp: 16 (over z, y, core).
Axes of the slice: x: 2, y: 2, z: 4, core: 2. Of those that a mesh axis runs over, the one named last changes fastest.
Arguments:
- x_tok: bfloat16 [256, 2048], P(('dp', 'cp')), parts along dimension 0
- prompt_lens: int32 [256], P('dp'), parts along dimension 0
- k_cache: bfloat16 [256, 1024, 2, 128], P('dp', 'cp'), parts along dimension 0
- v_cache: bfloat16 [256, 1024, 2, 128], P('dp', 'cp'), parts along dimension 0
- norm_gain: bfloat16 [2048], replicated
- w_q: bfloat16 [2048, 2048], replicated
- b_q: bfloat16 [2048], replicated
- w_k: bfloat16 [2048, 256], replicated
- b_k: bfloat16 [256], replicated
- w_v: bfloat16 [2048, 256], replicated
- b_v: bfloat16 [256], replicated
- w_o: bfloat16 [2048, 2048], replicated
Outputs:
- output 1: bfloat16 [256, 2048], P(('dp', 'cp')), parts along dimension 0
- output 2: bfloat16 [256, 1024, 2, 128], P(('dp', 'cp')), parts along dimension 0
- output 3: bfloat16 [256, 1024, 2, 128], P(('dp', 'cp')), parts along dimension 0
There are 2 independent parts. A program takes and returns all parts, laid end to end along the dimension named above; an argument that names none is the same for every part.
All inputs are finite; a program needn't handle non-finite values.
Results may differ from a plain program's by a relative error of at most 0.00668478.
Values are sent between devices in bfloat16 or wider.
A program may use at most 1 GiB of HBM per device.

v0:
```python
import jax
import jax.numpy as jnp
from jax import lax
from jax.sharding import PartitionSpec as P

RMS_EPS = 1e-6
ROPE_THETA = 1000000.0


def rotary(vectors, positions):
    head_dim = vectors.shape[-1]
    half_dim = head_dim // 2
    inv_freq = jnp.power(ROPE_THETA, -(jnp.arange(half_dim, dtype=jnp.float32) * 2.0 / head_dim))
    angle = positions.astype(jnp.float32)[:, None, None] * inv_freq
    cos_t = jnp.cos(angle)
    sin_t = jnp.sin(angle)
    first = vectors[..., :half_dim]
    second = vectors[..., half_dim:]
    return jnp.concatenate([first * cos_t - second * sin_t, second * cos_t + first * sin_t], axis=-1)


def project(x_tok, positions, norm_gain, w_q, b_q, w_k, b_k, w_v, b_v, head_dim):
    rows = x_tok.shape[0]
    x_wide = x_tok.astype(jnp.float32)
    mean_sq = jnp.mean(x_wide * x_wide, axis=-1, keepdims=True)
    normed = (x_wide * lax.rsqrt(mean_sq + RMS_EPS) * norm_gain.astype(jnp.float32)).astype(jnp.bfloat16)
    query = jnp.dot(normed, w_q, preferred_element_type=jnp.float32) + b_q.astype(jnp.float32)
    query = rotary(query.reshape(rows, -1, head_dim), positions).astype(jnp.bfloat16)
    key_new = jnp.dot(normed, w_k, preferred_element_type=jnp.float32) + b_k.astype(jnp.float32)
    key_new = rotary(key_new.reshape(rows, -1, head_dim), positions).astype(jnp.bfloat16)
    value_new = jnp.dot(normed, w_v, preferred_element_type=jnp.float32) + b_v.astype(jnp.float32)
    value_new = value_new.reshape(rows, -1, head_dim).astype(jnp.bfloat16)
    return query, key_new, value_new


def decode_local(x_tok, positions, keys_old, vals_old, norm_gain, w_q, b_q, w_k, b_k, w_v, b_v, w_o):
    rows, seq_len, kv_heads, head_dim = keys_old.shape
    query, key_new, value_new = project(x_tok, positions, norm_gain, w_q, b_q, w_k, b_k, w_v, b_v, head_dim)
    heads = query.shape[1]
    group = heads // kv_heads
    slot_idx = lax.broadcasted_iota(jnp.int32, (1, seq_len, 1, 1), 1)
    pos_col = positions[:, None, None, None]
    zero_val = jnp.zeros((), jnp.bfloat16)
    keys_all = jnp.where(slot_idx < pos_col, keys_old, jnp.where(slot_idx == pos_col, key_new[:, None], zero_val))
    vals_all = jnp.where(slot_idx < pos_col, vals_old, jnp.where(slot_idx == pos_col, value_new[:, None], zero_val))
    scores = jnp.einsum('bkgd,bskd->bkgs', query.reshape(rows, kv_heads, group, head_dim), keys_all, preferred_element_type=jnp.float32) * (head_dim ** -0.5)
    valid = lax.broadcasted_iota(jnp.int32, (1, 1, 1, seq_len), 3) <= pos_col
    scores = jnp.where(valid, scores, -1e30)
    row_max = jnp.max(scores, axis=-1, keepdims=True)
    weights = jnp.exp(scores - row_max)
    weight_sum = jnp.sum(weights, axis=-1, keepdims=True)
    mixed = jnp.einsum('bkgs,bskd->bkgd', weights.astype(jnp.bfloat16), vals_all, preferred_element_type=jnp.float32) / weight_sum
    attended = mixed.reshape(rows, heads * head_dim).astype(jnp.bfloat16)
    y_out = (x_tok.astype(jnp.float32) + jnp.dot(attended, w_o, preferred_element_type=jnp.float32)).astype(jnp.bfloat16)
    return y_out, keys_all, vals_all


def solution(mesh):
    batch_spec = P(('dp', 'cp'))
    seq_spec = P('dp', 'cp')
    whole = P()

    def per_device(x_tok, prompt_lens, k_cache, v_cache, norm_gain, w_q, b_q, w_k, b_k, w_v, b_v, w_o):
        rows = x_tok.shape[0]
        first_row = lax.axis_index('cp') * rows
        positions = lax.dynamic_slice_in_dim(prompt_lens, first_row, rows)
        keys_old = lax.all_to_all(k_cache, 'cp', 0, 1, tiled=True)
        vals_old = lax.all_to_all(v_cache, 'cp', 0, 1, tiled=True)
        return decode_local(x_tok, positions, keys_old, vals_old, norm_gain, w_q, b_q, w_k, b_k, w_v, b_v, w_o)

    return jax.shard_map(per_device, mesh=mesh, in_specs=(batch_spec, P('dp'), seq_spec, seq_spec, whole, whole, whole, whole, whole, whole, whole, whole), out_specs=(batch_spec, batch_spec, batch_spec), check_vma=False)
```

profile of v0, /device:TPU:13, one launch (start us, length us, event | category | flops | bytes accessed | tf_op | source)
XLA Modules:
  0.0 236.5 jit_solution(10078056192043680582)
XLA Ops:
  0.6 0.0 copy-start
  0.6 98.6 %all_to_all.36 = bf16[128,64,2,128]{3,2,1,0:T(2,128)(2,1)} all-to-all(bf16[128,64,2,128]{3,2,1,0:T(2,128)(2,1)} %param.14), channel_id=1, replica_groups=mesh['dp'=2,'cp'=16] {'cp'}, dimensions={0} | all-to-all | bytes 8388608 | tf_op jit(solution)/shard_map/all_to_all | solution.py:67
  99.3 0.0 copy-start.5
  99.3 0.0 copy-start.7
  99.3 5.6 %all-to-all-start.1 = ((bf16[128,64,2,128]{3,2,1,0:T(2,128)(2,1)}), bf16[128,64,2,128]{3,2,1,0:T(2,128)(2,1)}, u32[]{:S(2)}, u32[]{:S(2)}) async-start(bf16[128,64,2,128]{3,2,1,0:T(2,128)(2,1)} %param.15), calls=%async_computation.1 | async-start | bytes 8388608 | tf_op jit(solution)/shard_map/all_to_all | solution.py:68
  104.9 0.1 fusion.40
  105.0 0.1 fusion.28
  105.1 0.3 fusion.21
  105.4 0.1 multiply_cosine_fusion
  105.5 0.1 subtract_convert_fusion.1
  105.6 0.1 pad_maximum_fusion
  105.7 0.3 fusion.23
  106.0 0.1 iota_compare_fusion.2
  106.1 4.8 %fusion.11 = f32[8,16,128]{2,0,1:T(8,128)S(1)} fusion(bf16[2048,2048]{1,0:T(8,128)(2,1)} %param.17, f32[2048]{0:T(1024)S(1)} %convert_element_type.55, bf16[8,2048]{1,0:T(8,128)(2,1)S(1)} %copy-done.4, f32[2048]{0:T(1024)S(1)} %convert_element_type.53, f32[8]{0:T(128)S(1)} %add_rsqrt_fusion), kind=kOutput, calls=%fused_computation.13 | convolution fusion | flops 67190784 | bytes 8503328 | tf_op jit(solution)/shard_map/dot_general | solution.py:27
  110.9 0.1 subtract_convert_fusion
  111.0 6.0 %copy.17 = bf16[16,8,64,2,128]{4,3,2,0,1:T(2,128)(2,1)} copy(bf16[16,8,64,2,128]{4,3,2,1,0:T(2,128)(2,1)S(1)} %bitcast.32) | data formatting | bytes 8388608 | tf_op jit(solution)/shard_map/all_to_all | solution.py:67
  117.0 80.5 %all-to-all-done.1 = bf16[128,64,2,128]{3,2,1,0:T(2,128)(2,1)} async-done(((bf16[128,64,2,128]{3,2,1,0:T(2,128)(2,1)}), bf16[128,64,2,128]{3,2,1,0:T(2,128)(2,1)}, u32[]{:S(2)}, u32[]{:S(2)}) %all-to-all-start.1) | async-done | bytes 4194336 | tf_op jit(solution)/shard_map/all_to_all | solution.py:68
  197.5 11.8 %copy.20 = bf16[16,8,64,2,128]{4,3,2,0,1:T(2,128)(2,1)} copy(bf16[16,8,64,2,128]{4,3,2,1,0:T(2,128)(2,1)} %bitcast.7) | data formatting | bytes 8388608 | tf_op jit(solution)/shard_map/all_to_all | solution.py:68
  209.3 21.9 %broadcast_select_fusion.3 = (bf16[8,1024,2,128]{3,2,1,0:T(2,128)(2,1)S(1)}, bf16[8,1024,2,128]{3,2,1,0:T(2,128)(2,1)S(1)}) fusion(bf16[8,1024,2,128]{3,2,1,0:T(2,128)(2,1)} %bitcast.30, pred[8,1024]{1,0:T(8,128)(4,1)S(1)} %get-tuple-element.15, pred[8,1024]{1,0:T(8,128)(4,1)S(1)} %get-tuple-element.14, bf16[8,2,128]{2,1,0:T(2,128)(2,1)S(1)} %copy.18, ...), kind=kLoop, calls=%fused_computation.3 | loop fusion | flops 8388608 | bytes 16801792 | tf_op jit(solution)/shard_map/jit(_where)/select_n | solution.py:44
  231.3 1.3 fusion.41
  232.6 0.2 fusion.24
  232.9 0.8 fusion.18
  233.7 1.0 copy-done.3
  234.7 1.8 fusion.4
  (32 shorter events, 0.1 us)
Async XLA Ops:
  0.6 104.5 %copy-start = (bf16[2048,256]{1,0:T(8,128)(2,1)S(1)}, bf16[2048,256]{1,0:T(8,128)(2,1)}, u32[]{:S(2)}) copy-start(bf16[2048,256]{1,0:T(8,128)(2,1)} %param.19) | copy-start | bytes 3145732
  99.2 5.6 %copy-start.6 = (bf16[2048]{0:T(1024)(128)(2,1)S(1)}, bf16[2048]{0:T(1024)(128)(2,1)}, u32[]{:S(2)}) copy-start(bf16[2048]{0:T(1024)(128)(2,1)} %param.16) | copy-start | bytes 12292
  99.2 5.6 %copy-start.9 = (bf16[256]{0:T(256)(128)(2,1)S(1)}, bf16[256]{0:T(256)(128)(2,1)}, u32[]{:S(2)}) copy-start(bf16[256]{0:T(256)(128)(2,1)} %param.20) | copy-start | bytes 1540
  99.2 5.7 %copy-start.8 = (s32[128]{0:T(128)S(1)}, s32[128]{0:T(128)}, u32[]{:S(2)}) copy-start(s32[128]{0:T(128)} %param.13) | copy-start | bytes 1540
  99.2 5.7 %copy-start.4 = (bf16[8,2048]{1,0:T(8,128)(2,1)S(1)}, bf16[8,2048]{1,0:T(8,128)(2,1)}, u32[]{:S(2)}) copy-start(bf16[8,2048]{1,0:T(8,128)(2,1)} %param.12) | copy-start | bytes 98308
  99.2 6.5 %copy-start.10 = (bf16[256]{0:T(256)(128)(2,1)S(1)}, bf16[256]{0:T(256)(128)(2,1)}, u32[]{:S(2)}) copy-start(bf16[256]{0:T(256)(128)(2,1)} %param.22) | copy-start | bytes 1540
  99.3 6.5 %copy-start.5 = (bf16[2048,256]{1,0:T(8,128)(2,1)S(1)}, bf16[2048,256]{1,0:T(8,128)(2,1)}, u32[]{:S(2)}) copy-start(bf16[2048,256]{1,0:T(8,128)(2,1)} %param.21) | copy-start | bytes 3145732
  99.3 6.8 %copy-start.7 = (bf16[2048]{0:T(1024)(128)(2,1)S(1)}, bf16[2048]{0:T(1024)(128)(2,1)}, u32[]{:S(2)}) copy-start(bf16[2048]{0:T(1024)(128)(2,1)} %param.18) | copy-start | bytes 12292
  99.3 98.2 %all-to-all-start.1 = ((bf16[128,64,2,128]{3,2,1,0:T(2,128)(2,1)}), bf16[128,64,2,128]{3,2,1,0:T(2,128)(2,1)}, u32[]{:S(2)}, u32[]{:S(2)}) async-start(bf16[128,64,2,128]{3,2,1,0:T(2,128)(2,1)} %param.15), calls=%async_computation.1 | async-start | bytes 8388608 | tf_op jit(solution)/shard_map/all_to_all | solution.py:68
  106.1 4.9 %copy-start.2 = (bf16[128,64,2,128]{3,2,1,0:T(2,128)(2,1)S(1)}, bf16[128,64,2,128]{3,2,1,0:T(2,128)(2,1)}, u32[]{:S(2)}) copy-start(bf16[128,64,2,128]{3,2,1,0:T(2,128)(2,1)} %all_to_all.36) | copy-start | bytes 12582916
  197.5 37.1 %slice-start = ((s8[8388608]{0:T(1024)(128)(4,1)}), s8[4194304]{0:T(1024)(128)(4,1)S(1)}, s32[]{:S(2)}) async-start(s8[8388608]{0:T(1024)(128)(4,1)} %bitcast.28), calls=%async_computation.2 | async-start | bytes 8388608
  209.3 25.4 %slice-start.1 = ((s8[8388608]{0:T(1024)(128)(4,1)}), s8[4194304]{0:T(1024)(128)(4,1)S(1)}, s32[]{:S(2)}) async-start(s8[8388608]{0:T(1024)(128)(4,1)} %bitcast.28), calls=%async_computation.3 | async-start | bytes 8388608
  231.3 2.4 %copy-start.1 = (bf16[8,1024,2,128]{3,2,1,0:T(2,128)(2,1)}, bf16[8,1024,2,128]{3,2,1,0:T(2,128)(2,1)S(1)}, u32[]{:S(2)}) copy-start(bf16[8,1024,2,128]{3,2,1,0:T(2,128)(2,1)S(1)} %get-tuple-element.7) | copy-start | bytes 12582916
  231.3 3.4 %copy-start.3 = (bf16[8,1024,2,128]{3,2,1,0:T(2,128)(2,1)}, bf16[8,1024,2,128]{3,2,1,0:T(2,128)(2,1)S(1)}, u32[]{:S(2)}) copy-start(bf16[8,1024,2,128]{3,2,1,0:T(2,128)(2,1)S(1)} %get-tuple-element.8) | copy-start | bytes 12582916
where the time goes:
time: 237 us; the launch traced here: 236 us
  blocking collectives  98.6 us (42%)
  waiting for transfers between devices  80.5 us (34%)
  other arithmetic  22.9 us (10%)
  local copies, waits for them, and re-layouts  18.8 us (8%)
  matrix products  9.27 us (4%)
  starting transfers between devices  5.56 us (2%)
    all_to_all x1, blocking collectives, per_device(): keys_old = lax.all_to_all(k_cache, 'cp', 0, 1, tiled=True)  98.6 us
    all_to_all x1, waiting for transfers between devices, per_device(): vals_old = lax.all_to_all(v_cache, 'cp', 0, 1, tiled=True)  80.5 us
    select_n x1, other arithmetic, decode_local(): jnp.where(slot_idx < pos_col, keys_old, jnp.where(slot_idx == pos_col, ke...  21.9 us
    all_to_all x1, local copies, waits for them, and re-layouts, per_device(): vals_old = lax.all_to_all(v_cache, 'cp', 0, 1, tiled=True)  11.8 us
    all_to_all x1, local copies, waits for them, and re-layouts, per_device(): keys_old = lax.all_to_all(k_cache, 'cp', 0, 1, tiled=True)  6 us
    all_to_all x1, starting transfers between devices, per_device(): vals_old = lax.all_to_all(v_cache, 'cp', 0, 1, tiled=True)  5.56 us
    dot_general x1, matrix products, project(): jnp.dot(normed, w_q, preferred_element_type=jnp.float32)  4.76 us
  transfers between devices with their start and end apart: 1, of which 1 were waited for; matrix products, arithmetic and copies ran while one was open for 5% of the time, Pallas kernels for 0%

commit v1 on v0

v1 whole, which is shorter than its diff:
```python
import functools
import jax
import jax.numpy as jnp
from jax import lax
from jax.experimental import pallas as pl
from jax.experimental.pallas import tpu as pltpu
from jax.sharding import PartitionSpec as P

RMS_EPS = 1e-6
ROPE_THETA = 1000000.0
MESH = pl.DeviceIdType.MESH


def rotary(vectors, positions):
    head_dim = vectors.shape[-1]
    half_dim = head_dim // 2
    inv_freq = jnp.power(ROPE_THETA, -(jnp.arange(half_dim, dtype=jnp.float32) * 2.0 / head_dim))
    angle = positions.astype(jnp.float32)[:, None, None] * inv_freq
    cos_t = jnp.cos(angle)
    sin_t = jnp.sin(angle)
    first = vectors[..., :half_dim]
    second = vectors[..., half_dim:]
    return jnp.concatenate([first * cos_t - second * sin_t, second * cos_t + first * sin_t], axis=-1)


def project(x_tok, positions, norm_gain, w_q, b_q, w_k, b_k, w_v, b_v, head_dim):
    rows = x_tok.shape[0]
    x_wide = x_tok.astype(jnp.float32)
    mean_sq = jnp.mean(x_wide * x_wide, axis=-1, keepdims=True)
    normed = (x_wide * lax.rsqrt(mean_sq + RMS_EPS) * norm_gain.astype(jnp.float32)).astype(jnp.bfloat16)
    query = jnp.dot(normed, w_q, preferred_element_type=jnp.float32) + b_q.astype(jnp.float32)
    query = rotary(query.reshape(rows, -1, head_dim), positions).astype(jnp.bfloat16)
    key_new = jnp.dot(normed, w_k, preferred_element_type=jnp.float32) + b_k.astype(jnp.float32)
    key_new = rotary(key_new.reshape(rows, -1, head_dim), positions).astype(jnp.bfloat16)
    value_new = jnp.dot(normed, w_v, preferred_element_type=jnp.float32) + b_v.astype(jnp.float32)
    value_new = value_new.reshape(rows, -1, head_dim).astype(jnp.bfloat16)
    return query, key_new, value_new


def exchange_kernel(n, k_ref, v_ref, kr_ref, vr_ref, send_sem, recv_sem, local_sem):
    me = lax.axis_index("cp")
    barrier = pltpu.get_barrier_semaphore()

    def hello(d, c):
        pl.semaphore_signal(barrier, inc=1, device_id={"cp": lax.rem(me + d, n)}, device_id_type=MESH)
        return c

    lax.fori_loop(1, n, hello, 0)
    pl.semaphore_wait(barrier, n - 1)

    def remote(src, dst, a, d):
        to = lax.rem(me + d, n)
        return pltpu.make_async_remote_copy(
            src_ref=src.at[to], dst_ref=dst.at[:, me], send_sem=send_sem.at[a, d], recv_sem=recv_sem.at[a, d],
            device_id={"cp": to}, device_id_type=MESH)

    def start(d, c):
        remote(k_ref, kr_ref, 0, d).start()
        remote(v_ref, vr_ref, 1, d).start()
        return c

    lax.fori_loop(1, n, start, 0)
    own_k = pltpu.make_async_copy(k_ref.at[me], kr_ref.at[:, me], local_sem.at[0])
    own_v = pltpu.make_async_copy(v_ref.at[me], vr_ref.at[:, me], local_sem.at[1])
    own_k.start()
    own_v.start()

    def finish(d, c):
        remote(k_ref, kr_ref, 0, d).wait_send()
        remote(v_ref, vr_ref, 1, d).wait_send()
        src = lax.rem(me + n - d, n)
        pltpu.make_async_remote_copy(
            src_ref=k_ref.at[0], dst_ref=kr_ref.at[:, src], send_sem=send_sem.at[0, d], recv_sem=recv_sem.at[0, d],
            device_id={"cp": src}, device_id_type=MESH).wait_recv()
        pltpu.make_async_remote_copy(
            src_ref=v_ref.at[0], dst_ref=vr_ref.at[:, src], send_sem=send_sem.at[1, d], recv_sem=recv_sem.at[1, d],
            device_id={"cp": src}, device_id_type=MESH).wait_recv()
        return c

    lax.fori_loop(1, n, finish, 0)
    own_k.wait()
    own_v.wait()


def exchange(k, v):
    n, rows, m, d = k.shape
    out = jax.ShapeDtypeStruct((rows, n, m, d), k.dtype)
    return pl.pallas_call(
        functools.partial(exchange_kernel, n),
        out_shape=[out, out],
        in_specs=[pl.BlockSpec(memory_space=pl.ANY)] * 2,
        out_specs=[pl.BlockSpec(memory_space=pl.ANY)] * 2,
        scratch_shapes=[pltpu.SemaphoreType.DMA((2, n)), pltpu.SemaphoreType.DMA((2, n)), pltpu.SemaphoreType.DMA((2,))],
        compiler_params=pltpu.CompilerParams(collective_id=0, has_side_effects=True),
    )(k, v)


def attend_kernel(pos_ref, q_ref, kn_ref, vn_ref, kr_ref, vr_ref, ko_ref, vo_ref, o_ref):
    pos = pos_ref[pl.program_id(0)]
    heads, dim = q_ref.shape[1:]
    m = kr_ref.shape[1]
    row = lax.broadcasted_iota(jnp.int32, (m, dim), 0)
    zero = jnp.zeros((m, dim), jnp.float32)

    def merge(raw_ref, new_ref):
        new = new_ref[0].astype(jnp.float32)
        fresh = jnp.where(row % 2 == 0, new[0:1], new[1:2])
        return jnp.where(row < 2 * pos, raw_ref[0].astype(jnp.float32), jnp.where(row < 2 * pos + 2, fresh, zero)).astype(jnp.bfloat16)

    keys = merge(kr_ref, kn_ref)
    vals = merge(vr_ref, vn_ref)
    ko_ref[0] = keys
    vo_ref[0] = vals
    s = lax.dot_general(q_ref[0], keys, (((1,), (1,)), ((), ())), preferred_element_type=jnp.float32) * (dim ** -0.5)
    col = lax.broadcasted_iota(jnp.int32, (heads, m), 1)
    head = lax.broadcasted_iota(jnp.int32, (heads, m), 0)
    valid = (col < 2 * pos + 2) & (col % 2 == head // (heads // 2))
    s = jnp.where(valid, s, -1e30)
    top = jnp.max(s, axis=-1, keepdims=True)
    e = jnp.where(valid, jnp.exp(s - top), 0.0)
    total = jnp.sum(e, axis=-1, keepdims=True)
    o_ref[0] = (jnp.dot(e.astype(jnp.bfloat16), vals, preferred_element_type=jnp.float32) / total).astype(jnp.bfloat16)


def attend(positions, query, key_new, value_new, kr, vr):
    rows, heads, dim = query.shape
    m = kr.shape[1]
    big = pl.BlockSpec((1, m, dim), lambda b, p: (b, 0, 0))
    qs = pl.BlockSpec((1, heads, dim), lambda b, p: (b, 0, 0))
    ns = pl.BlockSpec((1, 2, dim), lambda b, p: (b, 0, 0))
    cache = jax.ShapeDtypeStruct(kr.shape, kr.dtype)
    return pl.pallas_call(
        attend_kernel,
        out_shape=[cache, cache, jax.ShapeDtypeStruct(query.shape, query.dtype)],
        grid_spec=pltpu.PrefetchScalarGridSpec(
            num_scalar_prefetch=1, grid=(rows,), in_specs=[qs, ns, ns, big, big], out_specs=[big, big, qs]),
    )(positions, query, key_new, value_new, kr, vr)


def solution(mesh):
    batch_spec = P(('dp', 'cp'))
    seq_spec = P('dp', 'cp')
    whole = P()

    def per_device(x_tok, prompt_lens, k_cache, v_cache, norm_gain, w_q, b_q, w_k, b_k, w_v, b_v, w_o):
        rows = x_tok.shape[0]
        batch, slots, kv_heads, dim = k_cache.shape
        n = batch // rows
        first_row = lax.axis_index('cp') * rows
        positions = lax.dynamic_slice_in_dim(prompt_lens, first_row, rows)
        query, key_new, value_new = project(x_tok, positions, norm_gain, w_q, b_q, w_k, b_k, w_v, b_v, dim)
        kr, vr = exchange(k_cache.reshape(n, rows, slots * kv_heads, dim), v_cache.reshape(n, rows, slots * kv_heads, dim))
        full = n * slots * kv_heads
        k_out, v_out, attended = attend(positions, query, key_new, value_new, kr.reshape(rows, full, dim), vr.reshape(rows, full, dim))
        attended = attended.reshape(rows, -1)
        y_out = (x_tok.astype(jnp.float32) + jnp.dot(attended, w_o, preferred_element_type=jnp.float32)).astype(jnp.bfloat16)
        shape = (rows, n * slots, kv_heads, dim)
        return y_out, k_out.reshape(shape), v_out.reshape(shape)

    return jax.shard_map(per_device, mesh=mesh, in_specs=(batch_spec, P('dp'), seq_spec, seq_spec, whole, whole, whole, whole, whole, whole, whole, whole), out_specs=(batch_spec, batch_spec, batch_spec), check_vma=False)
```

time: 237 us -> 218 us (0.920)
  the two profiles are of different devices: /device:TPU:13 before, /device:TPU:29 now
where the time goes in v1:
time: 218 us
  Pallas kernels  198 us (91%)
  matrix products  12.4 us (6%)
  other arithmetic  6.66 us (3%)
    pallas_call x1, Pallas kernels, exchange(): pl.pallas_call(functools.partial(exchange_kernel, n), out_shape=[out, out...  186 us
    pallas_call x1, Pallas kernels, attend(): pl.pallas_call(attend_kernel, out_shape=[cache, cache, jax.ShapeDtypeStru...  11.5 us
    dot_general x1, matrix products, per_device(): jnp.dot(attended, w_o, preferred_element_type=jnp.float32)  5.22 us
    dot_general x1, matrix products, project(): jnp.dot(normed, w_q, preferred_element_type=jnp.float32)  4.63 us

profile of v1, /device:TPU:29, one launch (start us, length us, event | category | flops | bytes accessed | tf_op | source)
XLA Modules:
  0.0 217.9 jit_solution(13754746452332723729)
XLA Ops:
  0.6 0.0 copy-start
  0.6 1.0 fusion.3
  1.6 1.3 fusion.11
  3.0 0.7 convert_element_type.38
  3.6 0.7 convert_element_type.39
  4.3 0.1 multiply_cosine_fusion
  4.4 0.7 convert_element_type.34
  5.1 0.0 copy-done
  5.1 1.0 fusion.2
  6.1 0.6 convert_element_type.41.vn_ref
  6.7 1.5 convolution_add_fusion.3
  8.3 0.1 subtract_convert_fusion.1
  8.4 0.7 pad_maximum_fusion.1.kn_ref
  9.0 0.7 convert_element_type.36
  9.7 4.6 %fusion.1 = f32[1,8,16,128]{3,1,2,0:T(8,128)S(1)} fusion(bf16[2048,2048]{1,0:T(8,128)(2,1)} %param.17, f32[2048]{0:T(1024)S(1)} %convert_element_type.36, bf16[8,2048]{1,0:T(8,128)(2,1)} %param.12, f32[2048]{0:T(1024)S(1)} %convert_element_type.34, f32[8]{0:T(128)S(1)} %add_rsqrt_fusion), kind=kOutput, calls=%fused_computation.3 | convolution fusion | flops 67190784 | bytes 8503328 | tf_op jit(solution)/shard_map/dot_general | solution.py:31
  14.4 0.1 subtract_convert_fusion
  14.5 0.7 pad_maximum_fusion.q_ref
  15.2 0.0 copy-start.1
  15.2 186.0 %shard_map.139 = (bf16[8,16,128,128]{3,2,1,0:T(8,128)(2,1)}, bf16[8,16,128,128]{3,2,1,0:T(8,128)(2,1)}) custom-call(bf16[16,8,128,128]{3,2,1,0:T(8,128)(2,1)} %bitcast.21, bf16[16,8,128,128]{3,2,1,0:T(8,128)(2,1)} %bitcast.22), custom_call_target="tpu_custom_call" | custom-call | tf_op jit(solution)/shard_map/pallas_call | solution.py:88
  201.2 11.5 %shard_map.140 = (bf16[8,2048,128]{2,1,0:T(8,128)(2,1)}, bf16[8,2048,128]{2,1,0:T(8,128)(2,1)}, bf16[8,16,128]{2,1,0:T(8,128)(2,1)}) custom-call(s32[8]{0:T(128)} %get-tuple-element.14.pos_ref, bf16[8,16,128]{2,1,0:T(8,128)(2,1)} %pad_maximum_fusion.q_ref, bf16[8,2,128]{2,1,0:T(2,128)(2,1)} %pad_maximum_fusion.1.kn_ref, ...), custom_call_target="tpu_custom_call" | custom-call | tf_op jit(solution)/shard_map/pallas_call | solution.py:132
  212.7 0.0 copy-done.1
  212.7 5.2 %fusion = bf16[8,2048]{1,0:T(8,128)(2,1)} fusion(bf16[2048,2048]{1,0:T(8,128)(2,1)} %param.23, bf16[8,2048]{1,0:T(8,128)(2,1)S(1)} %copy-done.1, bf16[1,8,16,128]{3,2,1,0:T(8,128)(2,1)} %bitcast.24), kind=kOutput, calls=%fused_computation.2 | convolution fusion | flops 67158016 | bytes 8486912 | tf_op jit(solution)/shard_map/dot_general | solution.py:156
  (4 shorter events, 0.0 us)
Async XLA Ops:
  0.6 4.5 %copy-start = (bf16[2048,256]{1,0:T(8,128)(2,1)S(1)}, bf16[2048,256]{1,0:T(8,128)(2,1)}, u32[]{:S(2)}) copy-start(bf16[2048,256]{1,0:T(8,128)(2,1)} %param.21) | copy-start | bytes 3145732
  15.2 197.5 %copy-start.1 = (bf16[8,2048]{1,0:T(8,128)(2,1)S(1)}, bf16[8,2048]{1,0:T(8,128)(2,1)}, u32[]{:S(2)}) copy-start(bf16[8,2048]{1,0:T(8,128)(2,1)} %param.12) | copy-start | bytes 98308

commit v2 on v0

v2 whole, which is shorter than its diff:
```python
import functools
import numpy as np
import jax
import jax.numpy as jnp
from jax import lax
from jax.experimental import pallas as pl
from jax.experimental.pallas import tpu as pltpu
from jax.sharding import PartitionSpec as P

RMS_EPS = 1e-6
ROPE_THETA = 1000000.0
MESH = pl.DeviceIdType.MESH
F32 = jnp.float32
BF16 = jnp.bfloat16


def flip(me, d):
    out = 0
    for k in range(4):
        bit = 1 << k
        out = out + bit * lax.rem(lax.div(me, bit) + lax.div(d, bit), 2)
    return out


def step_kernel(n, lens_ref, freq_ref, x_ref, gain_ref, bq_ref, bk_ref, bv_ref, wq_ref, wk_ref, wv_ref, wo_ref, k_ref, v_ref,
                att_ref, ko_ref, vo_ref, wo,
                k_land, v_land, wq, wk, wv, xs, gain, bq, bk, bv,
                q_s, kn_s, vn_s, s_s, e_s, l_s, acc, send_sem, recv_sem, load_sem):
    me = lax.axis_index("cp")
    rows, heads, dim = q_s.shape
    m = k_land.shape[2]
    width = heads * dim
    loads = {}
    for idx, (name, src, dst) in enumerate([
            ("x", x_ref, xs), ("gain", gain_ref, gain), ("bq", bq_ref, bq), ("bk", bk_ref, bk), ("bv", bv_ref, bv),
            ("wk", wk_ref, wk), ("wv", wv_ref, wv), ("wq", wq_ref, wq),
            ("k", k_ref.at[me], k_land.at[:, me]), ("v", v_ref.at[me], v_land.at[:, me]), ("wo", wo_ref, wo)]):
        loads[name] = pltpu.make_async_copy(src, dst, load_sem.at[idx])

    barrier = pltpu.get_barrier_semaphore()
    for d in range(1, n):
        pl.semaphore_signal(barrier, inc=1, device_id={"cp": lax.rem(me + d, n)}, device_id_type=MESH)
    for copy in loads.values():
        copy.start()
    pl.semaphore_wait(barrier, n - 1)

    pairs = ((k_ref, k_land), (v_ref, v_land))

    def send(a, d):
        to = flip(me, d)
        return pltpu.make_async_remote_copy(
            src_ref=pairs[a][0].at[to], dst_ref=pairs[a][1].at[:, me], send_sem=send_sem.at[a, d], recv_sem=recv_sem.at[a, me],
            device_id={"cp": to}, device_id_type=MESH)

    def arrive(a, d):
        src = flip(me, d)
        pltpu.make_async_remote_copy(
            src_ref=pairs[a][0].at[0], dst_ref=pairs[a][1].at[:, src], send_sem=send_sem.at[a, d], recv_sem=recv_sem.at[a, src],
            device_id={"cp": src}, device_id_type=MESH).wait_recv()
        return src

    order = (4, 5, 6, 7, 8, 9, 10, 11, 12, 13, 14, 15, 1, 2, 3)
    for a in range(2):
        for d in order:
            send(a, d).start()

    pos = [lens_ref[me * rows + b] for b in range(rows)]

    for name in ("x", "gain", "bq", "bk", "bv", "wk", "wv", "wq"):
        loads[name].wait()
    wide = xs[...].astype(F32)
    inv = lax.rsqrt(jnp.mean(wide * wide, axis=-1, keepdims=True) + RMS_EPS)
    gains = jnp.concatenate([gain[h:h + 1, :].astype(F32) for h in range(heads)], axis=1)
    normed = (wide * inv * gains).astype(BF16)
    which = lax.broadcasted_iota(jnp.int32, (rows, dim), 0)
    lane = lax.broadcasted_iota(jnp.int32, (rows, dim), 1)
    posf = jnp.zeros((rows, dim), F32)
    for b in range(rows):
        posf = jnp.where(which == b, pos[b].astype(F32), posf)
    angle = posf * freq_ref[...]
    cos_t = jnp.cos(angle)
    sin_t = jnp.sin(angle)
    sin_t = jnp.where(lane < dim // 2, -sin_t, sin_t)

    def rotate(t):
        return (t * cos_t + pltpu.roll(t, dim // 2, 1) * sin_t).astype(BF16).astype(F32)

    for h in range(2):
        cols = pl.ds(h * dim, dim)
        kn_s[:, h, :] = rotate(jnp.dot(normed, wk[:, cols], preferred_element_type=F32) + bk[h:h + 1, :].astype(F32))
        vn_s[:, h, :] = (jnp.dot(normed, wv[:, cols], preferred_element_type=F32) + bv[h:h + 1, :].astype(F32)).astype(BF16).astype(F32)
    for h in range(heads):
        q_s[:, h, :] = rotate(jnp.dot(normed, wq[:, h * dim:(h + 1) * dim], preferred_element_type=F32) + bq[h:h + 1, :].astype(F32))

    row = lax.broadcasted_iota(jnp.int32, (m, dim), 0)
    even = lax.rem(row, 2) == 0

    def merge(land, new, out, b, i):
        at = 2 * pos[b] - i * m
        fresh = jnp.where(even, new[b, 0:1, :], new[b, 1:2, :])
        merged = jnp.where(row < at, land[b, i].astype(F32), jnp.where(row < at + 2, fresh, 0.0)).astype(BF16)
        out[b, i] = merged
        return merged

    def k_block(i):
        cols = pl.ds(pl.multiple_of(i * m, m), m)
        for b in range(rows):
            keys = merge(k_land, kn_s, ko_ref, b, i)
            s_s[b, :, cols] = lax.dot_general(q_s[b].astype(BF16), keys, (((1,), (1,)), ((), ())), preferred_element_type=F32) * (dim ** -0.5)

    def v_block(i):
        cols = pl.ds(pl.multiple_of(i * m, m), m)
        for b in range(rows):
            vals = merge(v_land, vn_s, vo_ref, b, i)
            acc[b] += jnp.dot(e_s[b, :, cols], vals, preferred_element_type=F32)

    def k_step(d, c):
        k_block(arrive(0, d))
        return c

    def v_step(d, c):
        v_block(arrive(1, d))
        return c

    loads["k"].wait()
    k_block(me)
    lax.fori_loop(1, n, k_step, 0)

    col = lax.broadcasted_iota(jnp.int32, (heads, n * m), 1)
    head = lax.broadcasted_iota(jnp.int32, (heads, n * m), 0)
    mine = lax.rem(col, 2) == lax.div(head, heads // 2)
    for b in range(rows):
        valid = mine & (col < 2 * pos[b] + 2)
        s = jnp.where(valid, s_s[b], -1e30)
        e = jnp.where(valid, jnp.exp(s - jnp.max(s, axis=-1, keepdims=True)), 0.0)
        l_s[b] = jnp.broadcast_to(jnp.sum(e, axis=-1, keepdims=True), (heads, dim))
        e_s[b] = e.astype(BF16)
    acc[...] = jnp.zeros_like(acc)

    loads["v"].wait()
    v_block(me)
    loads["wo"].wait()
    lax.fori_loop(1, n, v_step, 0)

    acc[...] = acc[...] / l_s[...]
    att_ref[...] = jnp.concatenate([acc[:, h, :] for h in range(heads)], axis=1).astype(BF16)

    for a in range(2):
        for d in order:
            send(a, d).wait_send()


def step(lens, freq, x, gain, b_q, b_k, b_v, w_q, w_k, w_v, w_o, k, v):
    n, rows, m, dim = k.shape
    heads = w_q.shape[1] // dim
    kv = w_k.shape[1] // dim
    cache = pltpu.VMEM((rows, n, m, dim), BF16)
    hbm = pl.BlockSpec(memory_space=pltpu.HBM)
    vmem = pl.BlockSpec(memory_space=pltpu.VMEM)
    return pl.pallas_call(
        functools.partial(step_kernel, n),
        out_shape=[pltpu.VMEM(x.shape, BF16), cache, cache, pltpu.VMEM(w_o.shape, BF16)],
        in_specs=[pl.BlockSpec(memory_space=pltpu.SMEM), vmem] + [hbm] * 11,
        out_specs=[vmem] * 4,
        scratch_shapes=[
            pltpu.VMEM((rows, n, m, dim), BF16), pltpu.VMEM((rows, n, m, dim), BF16),
            pltpu.VMEM(w_q.shape, BF16), pltpu.VMEM(w_k.shape, BF16), pltpu.VMEM(w_v.shape, BF16),
            pltpu.VMEM(x.shape, BF16), pltpu.VMEM(gain.shape, BF16), pltpu.VMEM(b_q.shape, BF16), pltpu.VMEM(b_k.shape, BF16), pltpu.VMEM(b_v.shape, BF16),
            pltpu.VMEM((rows, heads, dim), F32), pltpu.VMEM((rows, kv, dim), F32), pltpu.VMEM((rows, kv, dim), F32),
            pltpu.VMEM((rows, heads, n * m), F32), pltpu.VMEM((rows, heads, n * m), BF16), pltpu.VMEM((rows, heads, dim), F32),
            pltpu.VMEM((rows, heads, dim), F32),
            pltpu.SemaphoreType.DMA((2, n)), pltpu.SemaphoreType.DMA((2, n)), pltpu.SemaphoreType.DMA((11,))],
        compiler_params=pltpu.CompilerParams(collective_id=0, has_side_effects=True, vmem_limit_bytes=47 * 1024 * 1024),
    )(lens, freq, x, gain, b_q, b_k, b_v, w_q, w_k, w_v, w_o, k, v)


def finish_kernel(x_ref, att_ref, wo_ref, k_ref, v_ref, y_ref, ko_ref, vo_ref, sem):
    copies = [pltpu.make_async_copy(k_ref, ko_ref, sem.at[0]), pltpu.make_async_copy(v_ref, vo_ref, sem.at[1])]
    for copy in copies:
        copy.start()
    tile = 256
    for t in range(wo_ref.shape[1] // tile):
        cols = slice(t * tile, (t + 1) * tile)
        y_ref[:, cols] = (x_ref[:, cols].astype(F32) + jnp.dot(att_ref[...], wo_ref[:, cols], preferred_element_type=F32)).astype(BF16)
    for copy in copies:
        copy.wait()


def finish(x, att, w_o, k, v):
    vmem = pl.BlockSpec(memory_space=pltpu.VMEM)
    hbm = pl.BlockSpec(memory_space=pltpu.HBM)
    cache = jax.ShapeDtypeStruct(k.shape, BF16)
    return pl.pallas_call(
        finish_kernel,
        out_shape=[jax.ShapeDtypeStruct(x.shape, BF16), cache, cache],
        in_specs=[vmem] * 5,
        out_specs=[vmem, hbm, hbm],
        scratch_shapes=[pltpu.SemaphoreType.DMA((2,))],
        compiler_params=pltpu.CompilerParams(vmem_limit_bytes=4 * 1024 * 1024),
    )(x, att, w_o, k, v)


def solution(mesh):
    batch_spec = P(('dp', 'cp'))
    seq_spec = P('dp', 'cp')
    whole = P()

    def per_device(x_tok, prompt_lens, k_cache, v_cache, norm_gain, w_q, b_q, w_k, b_k, w_v, b_v, w_o):
        rows = x_tok.shape[0]
        batch, slots, kv_heads, dim = k_cache.shape
        n = batch // rows
        inv_freq = np.power(np.float32(ROPE_THETA), -(np.arange(dim // 2, dtype=np.float32) * 2.0 / dim)).astype(np.float32)
        freq = jnp.asarray(np.concatenate([inv_freq, inv_freq])[None, :])
        pack = (n, rows, slots * kv_heads, dim)
        att, k_all, v_all, wo = step(
            prompt_lens, freq, x_tok, norm_gain.reshape(-1, dim), b_q.reshape(-1, dim), b_k.reshape(-1, dim), b_v.reshape(-1, dim),
            w_q, w_k, w_v, w_o, k_cache.reshape(pack), v_cache.reshape(pack))
        y_out, k_out, v_out = finish(x_tok, att, wo, k_all, v_all)
        shape = (rows, n * slots, kv_heads, dim)
        return y_out, k_out.reshape(shape), v_out.reshape(shape)

    return jax.shard_map(per_device, mesh=mesh, in_specs=(batch_spec, P('dp'), seq_spec, seq_spec, whole, whole, whole, whole, whole, whole, whole, whole), out_specs=(batch_spec, batch_spec, batch_spec), check_vma=False)
```

time: 237 us -> 202 us (0.85)
  the two profiles are of different devices: /device:TPU:13 before, /device:TPU:21 now
where the time goes in v2:
time: 202 us; the launch traced here: 201 us
  Pallas kernels  201 us (100%)
    pallas_call x1, Pallas kernels, step(): pl.pallas_call(functools.partial(step_kernel, n), out_shape=[pltpu.VMEM(x...  197 us
    pallas_call x1, Pallas kernels, finish(): pl.pallas_call(finish_kernel, out_shape=[jax.ShapeDtypeStruct(x.shape, BF...  4.07 us

profile of v2, /device:TPU:21, one launch (start us, length us, event | category | flops | bytes accessed | tf_op | source)
XLA Modules:
  0.0 201.3 jit_solution(620961932122987765)
XLA Ops:
  0.6 0.0 copy-start
  0.6 196.6 %shard_map.148 = (bf16[8,2048]{1,0:T(8,128)(2,1)S(1)}, bf16[8,16,128,128]{3,2,1,0:T(8,128)(2,1)S(1)}, bf16[8,16,128,128]{3,2,1,0:T(8,128)(2,1)S(1)}, bf16[2048,2048]{1,0:T(8,128)(2,1)S(1)}) custom-call(s32[128]{0:T(128)} %lens_ref.1, f32[1,128]{1,0:T(1,128)} %constant.2.clone.freq_ref, bf16[8,2048]{1,0:T(8,128)(2,1)} %x_ref.3, bf16[16,128]{1,0:T(8,128)(2,1)} %bitcast.10, ...), custom_call_target="tpu_custom_call" | custom-call | tf_op jit(solution)/shard_map/pallas_call | solution.py:160
  197.3 0.0 copy-done
  197.3 4.1 %shard_map.149 = (bf16[8,2048]{1,0:T(8,128)(2,1)}, bf16[8,16,128,128]{3,2,1,0:T(8,128)(2,1)}, bf16[8,16,128,128]{3,2,1,0:T(8,128)(2,1)}) custom-call(bf16[8,2048]{1,0:T(8,128)(2,1)S(1)} %copy-done, bf16[8,2048]{1,0:T(8,128)(2,1)S(1)} %get-tuple-element.10.att_ref, bf16[2048,2048]{1,0:T(8,128)(2,1)S(1)} %get-tuple-element.11.wo_ref, ...), custom_call_target="tpu_custom_call" | custom-call | tf_op jit(solution)/shard_map/pallas_call | solution.py:193
Async XLA Ops:
  0.6 196.6 %copy-start = (bf16[8,2048]{1,0:T(8,128)(2,1)S(1)}, bf16[8,2048]{1,0:T(8,128)(2,1)}, u32[]{:S(2)}) copy-start(bf16[8,2048]{1,0:T(8,128)(2,1)} %x_ref.3) | copy-start | bytes 98308

commit v3 on v2

--- a/solution.py
+++ b/solution.py
@@ -59,7 +59,7 @@
             device_id={"cp": src}, device_id_type=MESH).wait_recv()
         return src
 
-    order = (4, 5, 6, 7, 8, 9, 10, 11, 12, 13, 14, 15, 1, 2, 3)
+    order = (8, 9, 4, 10, 11, 5, 12, 13, 6, 14, 15, 7, 1, 2, 3)
     for a in range(2):
         for d in order:
             send(a, d).start()

time: 202 us -> 199 us (0.985)
  the two profiles are of different devices: /device:TPU:21 before, /device:TPU:13 now
where the time goes in v3:
time: 199 us; the launch traced here: 198 us
  Pallas kernels  198 us (99%)
    pallas_call x1, Pallas kernels, step(): pl.pallas_call(functools.partial(step_kernel, n), out_shape=[pltpu.VMEM(x...  194 us
    pallas_call x1, Pallas kernels, finish(): pl.pallas_call(finish_kernel, out_shape=[jax.ShapeDtypeStruct(x.shape, BF...  4.07 us

profile of v3, /device:TPU:13, one launch (start us, length us, event | category | flops | bytes accessed | tf_op | source)
XLA Modules:
  0.0 198.3 jit_solution(13772520375098215446)
XLA Ops:
  0.6 0.0 copy-start
  0.6 193.6 %shard_map.148 = (bf16[8,2048]{1,0:T(8,128)(2,1)S(1)}, bf16[8,16,128,128]{3,2,1,0:T(8,128)(2,1)S(1)}, bf16[8,16,128,128]{3,2,1,0:T(8,128)(2,1)S(1)}, bf16[2048,2048]{1,0:T(8,128)(2,1)S(1)}) custom-call(s32[128]{0:T(128)} %lens_ref.1, f32[1,128]{1,0:T(1,128)} %constant.2.clone.freq_ref, bf16[8,2048]{1,0:T(8,128)(2,1)} %x_ref.3, bf16[16,128]{1,0:T(8,128)(2,1)} %bitcast.10, ...), custom_call_target="tpu_custom_call" | custom-call | tf_op jit(solution)/shard_map/pallas_call | solution.py:160
  194.3 0.0 copy-done
  194.3 4.1 %shard_map.149 = (bf16[8,2048]{1,0:T(8,128)(2,1)}, bf16[8,16,128,128]{3,2,1,0:T(8,128)(2,1)}, bf16[8,16,128,128]{3,2,1,0:T(8,128)(2,1)}) custom-call(bf16[8,2048]{1,0:T(8,128)(2,1)S(1)} %copy-done, bf16[8,2048]{1,0:T(8,128)(2,1)S(1)} %get-tuple-element.10.att_ref, bf16[2048,2048]{1,0:T(8,128)(2,1)S(1)} %get-tuple-element.11.wo_ref, ...), custom_call_target="tpu_custom_call" | custom-call | tf_op jit(solution)/shard_map/pallas_call | solution.py:193
Async XLA Ops:
  0.6 193.6 %copy-start = (bf16[8,2048]{1,0:T(8,128)(2,1)S(1)}, bf16[8,2048]{1,0:T(8,128)(2,1)}, u32[]{:S(2)}) copy-start(bf16[8,2048]{1,0:T(8,128)(2,1)} %x_ref.3) | copy-start | bytes 98308

commit v4 on v3

--- a/solution.py
+++ b/solution.py
@@ -59,10 +59,14 @@
             device_id={"cp": src}, device_id_type=MESH).wait_recv()
         return src
 
-    order = (8, 9, 4, 10, 11, 5, 12, 13, 6, 14, 15, 7, 1, 2, 3)
-    for a in range(2):
-        for d in order:
-            send(a, d).start()
+    near, far, beside = (4, 5, 6, 7), (8, 9, 10, 11, 12, 13, 14, 15), (1, 2, 3)
+    plan = [(0, d, d + 8) for d in near] + [(1, d, d + 8) for d in near]
+    plan += [(a, d, e) for a in range(2) for d, e in zip(far, (8, 9, 4, 10, 11, 5, 6, 7))]
+    plan += [(a, d, d) for a in range(2) for d in beside]
+    end = lax.rem(lax.div(lax.div(me, 4) + 1, 2) + 1, 2)
+    plan = [(a, e + end * (d - e)) for a, d, e in plan]
+    for a, d in plan:
+        send(a, d).start()
 
     pos = [lens_ref[me * rows + b] for b in range(rows)]
 
@@ -145,9 +149,8 @@
     acc[...] = acc[...] / l_s[...]
     att_ref[...] = jnp.concatenate([acc[:, h, :] for h in range(heads)], axis=1).astype(BF16)
 
-    for a in range(2):
-        for d in order:
-            send(a, d).wait_send()
+    for a, d in plan:
+        send(a, d).wait_send()
 
 
 def step(lens, freq, x, gain, b_q, b_k, b_v, w_q, w_k, w_v, w_o, k, v):

time: 199 us -> 213 us (1.070)
  the two profiles are of different devices: /device:TPU:13 before, /device:TPU:0 now
where the time goes in v4:
time: 213 us; the launch traced here: 212 us
  Pallas kernels  211 us (99%)
    pallas_call x1, Pallas kernels, step(): pl.pallas_call(functools.partial(step_kernel, n), out_shape=[pltpu.VMEM(x...  207 us

profile of v4, /device:TPU:0, one launch (start us, length us, event | category | flops | bytes accessed | tf_op | source)
XLA Modules:
  0.0 211.9 jit_solution(7613329549123984697)
XLA Ops:
  0.6 0.0 copy-start
  0.6 207.1 %shard_map.148 = (bf16[8,2048]{1,0:T(8,128)(2,1)S(1)}, bf16[8,16,128,128]{3,2,1,0:T(8,128)(2,1)S(1)}, bf16[8,16,128,128]{3,2,1,0:T(8,128)(2,1)S(1)}, bf16[2048,2048]{1,0:T(8,128)(2,1)S(1)}) custom-call(s32[128]{0:T(128)} %lens_ref.1, f32[1,128]{1,0:T(1,128)} %constant.2.clone.freq_ref, bf16[8,2048]{1,0:T(8,128)(2,1)} %x_ref.3, bf16[16,128]{1,0:T(8,128)(2,1)} %bitcast.10, ...), custom_call_target="tpu_custom_call" | custom-call | tf_op jit(solution)/shard_map/pallas_call | solution.py:163
  207.8 0.0 copy-done
  207.8 4.1 %shard_map.149 = (bf16[8,2048]{1,0:T(8,128)(2,1)}, bf16[8,16,128,128]{3,2,1,0:T(8,128)(2,1)}, bf16[8,16,128,128]{3,2,1,0:T(8,128)(2,1)}) custom-call(bf16[8,2048]{1,0:T(8,128)(2,1)S(1)} %copy-done, bf16[8,2048]{1,0:T(8,128)(2,1)S(1)} %get-tuple-element.10.att_ref, bf16[2048,2048]{1,0:T(8,128)(2,1)S(1)} %get-tuple-element.11.wo_ref, ...), custom_call_target="tpu_custom_call" | custom-call | tf_op jit(solution)/shard_map/pallas_call | solution.py:196
Async XLA Ops:
  0.6 207.2 %copy-start = (bf16[8,2048]{1,0:T(8,128)(2,1)S(1)}, bf16[8,2048]{1,0:T(8,128)(2,1)}, u32[]{:S(2)}) copy-start(bf16[8,2048]{1,0:T(8,128)(2,1)} %x_ref.3) | copy-start | bytes 98308

commit v5 on v4

--- a/solution.py
+++ b/solution.py
@@ -47,24 +47,19 @@
     pairs = ((k_ref, k_land), (v_ref, v_land))
 
     def send(a, d):
-        to = flip(me, d)
+        to = lax.rem(me + d, n)
         return pltpu.make_async_remote_copy(
             src_ref=pairs[a][0].at[to], dst_ref=pairs[a][1].at[:, me], send_sem=send_sem.at[a, d], recv_sem=recv_sem.at[a, me],
             device_id={"cp": to}, device_id_type=MESH)
 
     def arrive(a, d):
-        src = flip(me, d)
+        src = lax.rem(me + n - d, n)
         pltpu.make_async_remote_copy(
             src_ref=pairs[a][0].at[0], dst_ref=pairs[a][1].at[:, src], send_sem=send_sem.at[a, d], recv_sem=recv_sem.at[a, src],
             device_id={"cp": src}, device_id_type=MESH).wait_recv()
         return src
 
-    near, far, beside = (4, 5, 6, 7), (8, 9, 10, 11, 12, 13, 14, 15), (1, 2, 3)
-    plan = [(0, d, d + 8) for d in near] + [(1, d, d + 8) for d in near]
-    plan += [(a, d, e) for a in range(2) for d, e in zip(far, (8, 9, 4, 10, 11, 5, 6, 7))]
-    plan += [(a, d, d) for a in range(2) for d in beside]
-    end = lax.rem(lax.div(lax.div(me, 4) + 1, 2) + 1, 2)
-    plan = [(a, e + end * (d - e)) for a, d, e in plan]
+    plan = [(a, d) for d in range(1, n) for a in range(2)]
     for a, d in plan:
         send(a, d).start()
 

time: 213 us -> 193 us (0.906)
  the two profiles are of different devices: /device:TPU:0 before, /device:TPU:29 now
where the time goes in v5:
time: 193 us
  Pallas kernels  193 us (100%)
    pallas_call x1, Pallas kernels, step(): pl.pallas_call(functools.partial(step_kernel, n), out_shape=[pltpu.VMEM(x...  188 us
    pallas_call x1, Pallas kernels, finish(): pl.pallas_call(finish_kernel, out_shape=[jax.ShapeDtypeStruct(x.shape, BF...  4.07 us

profile of v5, /device:TPU:29, one launch (start us, length us, event | category | flops | bytes accessed | tf_op | source)
XLA Modules:
  0.0 193.2 jit_solution(3091394923577480132)
XLA Ops:
  0.6 0.0 copy-start
  0.6 188.5 %shard_map.148 = (bf16[8,2048]{1,0:T(8,128)(2,1)S(1)}, bf16[8,16,128,128]{3,2,1,0:T(8,128)(2,1)S(1)}, bf16[8,16,128,128]{3,2,1,0:T(8,128)(2,1)S(1)}, bf16[2048,2048]{1,0:T(8,128)(2,1)S(1)}) custom-call(s32[128]{0:T(128)} %lens_ref.1, f32[1,128]{1,0:T(1,128)} %constant.2.clone.freq_ref, bf16[8,2048]{1,0:T(8,128)(2,1)} %x_ref.3, bf16[16,128]{1,0:T(8,128)(2,1)} %bitcast.10, ...), custom_call_target="tpu_custom_call" | custom-call | tf_op jit(solution)/shard_map/pallas_call | solution.py:158
  189.1 0.0 copy-done
  189.1 4.1 %shard_map.149 = (bf16[8,2048]{1,0:T(8,128)(2,1)}, bf16[8,16,128,128]{3,2,1,0:T(8,128)(2,1)}, bf16[8,16,128,128]{3,2,1,0:T(8,128)(2,1)}) custom-call(bf16[8,2048]{1,0:T(8,128)(2,1)S(1)} %copy-done, bf16[8,2048]{1,0:T(8,128)(2,1)S(1)} %get-tuple-element.10.att_ref, bf16[2048,2048]{1,0:T(8,128)(2,1)S(1)} %get-tuple-element.11.wo_ref, ...), custom_call_target="tpu_custom_call" | custom-call | tf_op jit(solution)/shard_map/pallas_call | solution.py:191
Async XLA Ops:
  0.6 188.5 %copy-start = (bf16[8,2048]{1,0:T(8,128)(2,1)S(1)}, bf16[8,2048]{1,0:T(8,128)(2,1)}, u32[]{:S(2)}) copy-start(bf16[8,2048]{1,0:T(8,128)(2,1)} %x_ref.3) | copy-start | bytes 98308

commit v6 on v5

--- a/solution.py
+++ b/solution.py
@@ -47,19 +47,19 @@
     pairs = ((k_ref, k_land), (v_ref, v_land))
 
     def send(a, d):
-        to = lax.rem(me + d, n)
+        to = flip(me, d)
         return pltpu.make_async_remote_copy(
             src_ref=pairs[a][0].at[to], dst_ref=pairs[a][1].at[:, me], send_sem=send_sem.at[a, d], recv_sem=recv_sem.at[a, me],
             device_id={"cp": to}, device_id_type=MESH)
 
     def arrive(a, d):
-        src = lax.rem(me + n - d, n)
+        src = flip(me, d)
         pltpu.make_async_remote_copy(
             src_ref=pairs[a][0].at[0], dst_ref=pairs[a][1].at[:, src], send_sem=send_sem.at[a, d], recv_sem=recv_sem.at[a, src],
             device_id={"cp": src}, device_id_type=MESH).wait_recv()
         return src
 
-    plan = [(a, d) for d in range(1, n) for a in range(2)]
+    plan = [(a, d) for a in range(2) for d in (8, 4, 9, 1, 10, 5, 11, 2, 12, 6, 13, 3, 14, 7, 15)]
     for a, d in plan:
         send(a, d).start()
 
@@ -173,7 +173,7 @@
 
 
 def finish_kernel(x_ref, att_ref, wo_ref, k_ref, v_ref, y_ref, ko_ref, vo_ref, sem):
-    copies = [pltpu.make_async_copy(k_ref, ko_ref, sem.at[0]), pltpu.make_async_copy(v_ref, vo_ref, sem.at[1])]
+    copies = [pltpu.make_async_copy(src.at[b], dst.at[b], sem.at[a, b]) for a, (src, dst) in enumerate(((k_ref, ko_ref), (v_ref, vo_ref))) for b in range(k_ref.shape[0])]
     for copy in copies:
         copy.start()
     tile = 256
@@ -193,7 +193,7 @@
         out_shape=[jax.ShapeDtypeStruct(x.shape, BF16), cache, cache],
         in_specs=[vmem] * 5,
         out_specs=[vmem, hbm, hbm],
-        scratch_shapes=[pltpu.SemaphoreType.DMA((2,))],
+        scratch_shapes=[pltpu.SemaphoreType.DMA((2, k.shape[0]))],
         compiler_params=pltpu.CompilerParams(vmem_limit_bytes=4 * 1024 * 1024),
     )(x, att, w_o, k, v)
 

time: 193 us -> 198 us (1.026)
  the two profiles are of different devices: /device:TPU:29 before, /device:TPU:21 now
where the time goes in v6:
time: 198 us; the launch traced here: 197 us
  Pallas kernels  197 us (99%)
    pallas_call x1, Pallas kernels, step(): pl.pallas_call(functools.partial(step_kernel, n), out_shape=[pltpu.VMEM(x...  192 us
    pallas_call x1, Pallas kernels, finish(): pl.pallas_call(finish_kernel, out_shape=[jax.ShapeDtypeStruct(x.shape, BF...  4.93 us

profile of v6, /device:TPU:21, one launch (start us, length us, event | category | flops | bytes accessed | tf_op | source)
XLA Modules:
  0.0 197.4 jit_solution(3820097339160516269)
XLA Ops:
  0.6 0.0 copy-start
  0.6 191.8 %shard_map.148 = (bf16[8,2048]{1,0:T(8,128)(2,1)S(1)}, bf16[8,16,128,128]{3,2,1,0:T(8,128)(2,1)S(1)}, bf16[8,16,128,128]{3,2,1,0:T(8,128)(2,1)S(1)}, bf16[2048,2048]{1,0:T(8,128)(2,1)S(1)}) custom-call(s32[128]{0:T(128)} %lens_ref.1, f32[1,128]{1,0:T(1,128)} %constant.2.clone.freq_ref, bf16[8,2048]{1,0:T(8,128)(2,1)} %x_ref.3, bf16[16,128]{1,0:T(8,128)(2,1)} %bitcast.10, ...), custom_call_target="tpu_custom_call" | custom-call | tf_op jit(solution)/shard_map/pallas_call | solution.py:158
  192.5 0.0 copy-done
  192.5 4.9 %shard_map.149 = (bf16[8,2048]{1,0:T(8,128)(2,1)}, bf16[8,16,128,128]{3,2,1,0:T(8,128)(2,1)}, bf16[8,16,128,128]{3,2,1,0:T(8,128)(2,1)}) custom-call(bf16[8,2048]{1,0:T(8,128)(2,1)S(1)} %copy-done, bf16[8,2048]{1,0:T(8,128)(2,1)S(1)} %get-tuple-element.10.att_ref, bf16[2048,2048]{1,0:T(8,128)(2,1)S(1)} %get-tuple-element.11.wo_ref, ...), custom_call_target="tpu_custom_call" | custom-call | tf_op jit(solution)/shard_map/pallas_call | solution.py:191
Async XLA Ops:
  0.6 191.8 %copy-start = (bf16[8,2048]{1,0:T(8,128)(2,1)S(1)}, bf16[8,2048]{1,0:T(8,128)(2,1)}, u32[]{:S(2)}) copy-start(bf16[8,2048]{1,0:T(8,128)(2,1)} %x_ref.3) | copy-start | bytes 98308

commit v7 on v5

--- a/solution.py
+++ b/solution.py
@@ -22,9 +22,9 @@
     return out
 
 
-def step_kernel(n, lens_ref, freq_ref, x_ref, gain_ref, bq_ref, bk_ref, bv_ref, wq_ref, wk_ref, wv_ref, wo_ref, k_ref, v_ref,
+def step_kernel(n, lens_hbm, freq_hbm, x_ref, gain_ref, bq_ref, bk_ref, bv_ref, wq_ref, wk_ref, wv_ref, wo_ref, k_ref, v_ref,
                 att_ref, ko_ref, vo_ref, wo,
-                k_land, v_land, wq, wk, wv, xs, gain, bq, bk, bv,
+                lens_ref, freq_ref, k_land, v_land, wq, wk, wv, xs, gain, bq, bk, bv,
                 q_s, kn_s, vn_s, s_s, e_s, l_s, acc, send_sem, recv_sem, load_sem):
     me = lax.axis_index("cp")
     rows, heads, dim = q_s.shape
@@ -32,7 +32,7 @@
     width = heads * dim
     loads = {}
     for idx, (name, src, dst) in enumerate([
-            ("x", x_ref, xs), ("gain", gain_ref, gain), ("bq", bq_ref, bq), ("bk", bk_ref, bk), ("bv", bv_ref, bv),
+            ("lens", lens_hbm, lens_ref), ("freq", freq_hbm, freq_ref), ("x", x_ref, xs), ("gain", gain_ref, gain), ("bq", bq_ref, bq), ("bk", bk_ref, bk), ("bv", bv_ref, bv),
             ("wk", wk_ref, wk), ("wv", wv_ref, wv), ("wq", wq_ref, wq),
             ("k", k_ref.at[me], k_land.at[:, me]), ("v", v_ref.at[me], v_land.at[:, me]), ("wo", wo_ref, wo)]):
         loads[name] = pltpu.make_async_copy(src, dst, load_sem.at[idx])
@@ -63,9 +63,10 @@
     for a, d in plan:
         send(a, d).start()
 
+    loads["lens"].wait()
     pos = [lens_ref[me * rows + b] for b in range(rows)]
 
-    for name in ("x", "gain", "bq", "bk", "bv", "wk", "wv", "wq"):
+    for name in ("freq", "x", "gain", "bq", "bk", "bv", "wk", "wv", "wq"):
         loads[name].wait()
     wide = xs[...].astype(F32)
     inv = lax.rsqrt(jnp.mean(wide * wide, axis=-1, keepdims=True) + RMS_EPS)
@@ -158,16 +159,17 @@
     return pl.pallas_call(
         functools.partial(step_kernel, n),
         out_shape=[pltpu.VMEM(x.shape, BF16), cache, cache, pltpu.VMEM(w_o.shape, BF16)],
-        in_specs=[pl.BlockSpec(memory_space=pltpu.SMEM), vmem] + [hbm] * 11,
+        in_specs=[hbm] * 13,
         out_specs=[vmem] * 4,
         scratch_shapes=[
+            pltpu.SMEM(lens.shape, jnp.int32), pltpu.VMEM(freq.shape, F32),
             pltpu.VMEM((rows, n, m, dim), BF16), pltpu.VMEM((rows, n, m, dim), BF16),
             pltpu.VMEM(w_q.shape, BF16), pltpu.VMEM(w_k.shape, BF16), pltpu.VMEM(w_v.shape, BF16),
             pltpu.VMEM(x.shape, BF16), pltpu.VMEM(gain.shape, BF16), pltpu.VMEM(b_q.shape, BF16), pltpu.VMEM(b_k.shape, BF16), pltpu.VMEM(b_v.shape, BF16),
             pltpu.VMEM((rows, heads, dim), F32), pltpu.VMEM((rows, kv, dim), F32), pltpu.VMEM((rows, kv, dim), F32),
             pltpu.VMEM((rows, heads, n * m), F32), pltpu.VMEM((rows, heads, n * m), BF16), pltpu.VMEM((rows, heads, dim), F32),
             pltpu.VMEM((rows, heads, dim), F32),
-            pltpu.SemaphoreType.DMA((2, n)), pltpu.SemaphoreType.DMA((2, n)), pltpu.SemaphoreType.DMA((11,))],
+            pltpu.SemaphoreType.DMA((2, n)), pltpu.SemaphoreType.DMA((2, n)), pltpu.SemaphoreType.DMA((13,))],
         compiler_params=pltpu.CompilerParams(collective_id=0, has_side_effects=True, vmem_limit_bytes=47 * 1024 * 1024),
     )(lens, freq, x, gain, b_q, b_k, b_v, w_q, w_k, w_v, w_o, k, v)
 

time: 193 us -> 193 us (level)
  no operation moved by 1% of the time
where the time goes in v7:
time: 193 us; the launch traced here: 192 us
  Pallas kernels  192 us (99%)
    pallas_call x1, Pallas kernels, step(): pl.pallas_call(functools.partial(step_kernel, n), out_shape=[pltpu.VMEM(x...  188 us
    pallas_call x1, Pallas kernels, finish(): pl.pallas_call(finish_kernel, out_shape=[jax.ShapeDtypeStruct(x.shape, BF...  4.07 us

profile of v7, /device:TPU:29, one launch (start us, length us, event | category | flops | bytes accessed | tf_op | source)
XLA Modules:
  0.0 192.4 jit_solution(3934336669918524643)
XLA Ops:
  0.6 0.0 copy-start
  0.6 187.7 %shard_map.148 = (bf16[8,2048]{1,0:T(8,128)(2,1)S(1)}, bf16[8,16,128,128]{3,2,1,0:T(8,128)(2,1)S(1)}, bf16[8,16,128,128]{3,2,1,0:T(8,128)(2,1)S(1)}, bf16[2048,2048]{1,0:T(8,128)(2,1)S(1)}) custom-call(s32[128]{0:T(128)} %lens_hbm.1, f32[1,128]{1,0:T(1,128)} %constant.2.clone.freq_hbm, bf16[8,2048]{1,0:T(8,128)(2,1)} %x_ref.3, bf16[16,128]{1,0:T(8,128)(2,1)} %bitcast.10, ...), custom_call_target="tpu_custom_call" | custom-call | tf_op jit(solution)/shard_map/pallas_call | solution.py:159
  188.3 0.0 copy-done
  188.3 4.1 %shard_map.149 = (bf16[8,2048]{1,0:T(8,128)(2,1)}, bf16[8,16,128,128]{3,2,1,0:T(8,128)(2,1)}, bf16[8,16,128,128]{3,2,1,0:T(8,128)(2,1)}) custom-call(bf16[8,2048]{1,0:T(8,128)(2,1)S(1)} %copy-done, bf16[8,2048]{1,0:T(8,128)(2,1)S(1)} %get-tuple-element.10.att_ref, bf16[2048,2048]{1,0:T(8,128)(2,1)S(1)} %get-tuple-element.11.wo_ref, ...), custom_call_target="tpu_custom_call" | custom-call | tf_op jit(solution)/shard_map/pallas_call | solution.py:193
Async XLA Ops:
  0.6 187.7 %copy-start = (bf16[8,2048]{1,0:T(8,128)(2,1)S(1)}, bf16[8,2048]{1,0:T(8,128)(2,1)}, u32[]{:S(2)}) copy-start(bf16[8,2048]{1,0:T(8,128)(2,1)} %x_ref.3) | copy-start | bytes 98308

commit v8 on v7

v8 whole, which is shorter than its diff:
```python
import functools
import numpy as np
import jax
import jax.numpy as jnp
from jax import lax
from jax.experimental import pallas as pl
from jax.experimental.pallas import tpu as pltpu
from jax.sharding import PartitionSpec as P

RMS_EPS = 1e-6
ROPE_THETA = 1000000.0
MESH = pl.DeviceIdType.MESH
F32 = jnp.float32
BF16 = jnp.bfloat16


def flip(me, d):
    out = 0
    for k in range(4):
        bit = 1 << k
        out = out + bit * lax.rem(lax.div(me, bit) + lax.div(d, bit), 2)
    return out


PIECE = (7, 7, 6, 6)


def step_kernel(n, pooled, lens_hbm, freq_hbm, x_ref, gain_ref, bq_ref, bk_ref, bv_ref, wq_ref, wk_ref, wv_ref, wo_ref, k_ref, v_ref,
                att_ref, ko_ref, vo_ref, wo,
                lens_ref, freq_ref, k_land, v_land, wq, wk, wv, xs, gain, bq, bk, bv,
                q_s, kn_s, vn_s, s_s, e_s, l_s, acc, send_sem, recv_sem, load_sem, *pool):
    me = lax.axis_index("cp")
    rows, heads, dim = q_s.shape
    m = k_land.shape[2]
    half = n // 2
    high = lax.div(me, half)
    h = lax.rem(me, half)
    other = (1 - high) * half
    inner = lax.rem(lax.div(me, 4) + high, 2) == 1
    outer = lax.rem(lax.div(me, 4) + high, 2) == 0
    loads = {}
    for idx, (name, src, dst) in enumerate([
            ("lens", lens_hbm, lens_ref), ("freq", freq_hbm, freq_ref), ("x", x_ref, xs), ("gain", gain_ref, gain), ("bq", bq_ref, bq), ("bk", bk_ref, bk), ("bv", bv_ref, bv),
            ("wk", wk_ref, wk), ("wv", wv_ref, wv), ("wq", wq_ref, wq),
            ("k", k_ref.at[me], k_land.at[:, me]), ("v", v_ref.at[me], v_land.at[:, me]), ("wo", wo_ref, wo)]):
        loads[name] = pltpu.make_async_copy(src, dst, load_sem.at[idx])

    pairs = ((k_ref, k_land), (v_ref, v_land))

    def send(a, to):
        return pltpu.make_async_remote_copy(
            src_ref=pairs[a][0].at[to], dst_ref=pairs[a][1].at[:, me], send_sem=send_sem.at[a, to], recv_sem=recv_sem.at[a, me],
            device_id={"cp": to}, device_id_type=MESH)

    def arrive(a, src):
        pltpu.make_async_remote_copy(
            src_ref=pairs[a][0].at[0], dst_ref=pairs[a][1].at[:, src], send_sem=send_sem.at[a, src], recv_sem=recv_sem.at[a, src],
            device_id={"cp": src}, device_id_type=MESH).wait_recv()

    def both(to, act):
        for a in range(2):
            act(send(a, to))

    def start(copy):
        copy.start()

    def sent(copy):
        copy.wait_send()

    barrier = pltpu.get_barrier_semaphore()
    for d in range(1, n):
        pl.semaphore_signal(barrier, inc=1, device_id={"cp": lax.rem(me + d, n)}, device_id_type=MESH)
    loads["lens"].start()
    if pooled:
        (k_all, v_all, k_pack, v_pack, next_s, pick_s, place_s, gather_sem, st_send, st_recv, fw_send, fw_recv), land = pool[:12], (pool[12:16], pool[16:20])
        caches, packs = (k_all, v_all), (k_pack, v_pack)

        def gather(a, j):
            return pltpu.make_async_copy(pairs[a][0].at[other + j], caches[a].at[pl.ds(j * rows, rows)], gather_sem.at[a, j])

        @pl.when(inner)
        def _():
            for a in range(2):
                for j in range(half):
                    gather(a, j).start()

    for name, copy in loads.items():
        if name != "lens":
            copy.start()
    pl.semaphore_wait(barrier, n - 1)

    if not pooled:
        for d in range(1, n):
            both(lax.rem(me + d, n), start)
        loads["lens"].wait()
    else:
        near = [high * half + lax.rem(h + t, half) for t in range(1, half)]
        far = [other + lax.rem(h + t, half) for t in range(half)]
        beside = [lax.div(to, 4) == lax.div(me, 4) for to in near]
        apart = [lax.div(to, 4) != lax.div(me, 4) for to in near]
        for to, ok in zip(near, beside):
            @pl.when(outer | ok)
            def _():
                both(to, start)

        @pl.when(outer)
        def _():
            send(0, far[0]).start()

        loads["lens"].wait()
        mine = jnp.where(lax.rem(me, 4) < 2, PIECE[0], PIECE[2])

        @pl.when(inner)
        def _():
            next_s[half * rows] = half * rows

            def back(t, carry):
                b = half * rows - 1 - t
                nx = jnp.where(lens_ref[other * rows + b] > (m // 2) * me, b, carry)
                next_s[b] = nx
                return nx

            lax.fori_loop(0, half * rows, back, half * rows, unroll=8)

            def fill(s, cur):
                cand = next_s[cur]
                ok = s >= (lax.shift_right_logical(cand, 3) - 1) * mine
                pick_s[s] = jnp.minimum(cand, half * rows - 1)
                return jnp.where(ok, jnp.minimum(cand + 1, half * rows), cur)

            lax.fori_loop(0, half * max(PIECE), fill, 0, unroll=8)
            for a in range(2):
                for j in range(half):
                    gather(a, j).wait()

            def pack(s, c):
                b = pick_s[s]
                for a in range(2):
                    packs[a][s] = caches[a][b]
                return c

            lax.fori_loop(0, half * max(PIECE), pack, 0, unroll=4)

        def place(b, ends):
            length = lens_ref[high * half * rows + b]
            out = []
            for u in range(4):
                at = jnp.maximum(ends[u], (lax.div(b, rows) - 1) * PIECE[u])
                place_s[u, b] = at
                out.append(jnp.where(length > (m // 2) * (half - 4 * high + u), at + 1, ends[u]))
            return tuple(out)

        lax.fori_loop(0, half * rows, place, (0, 0, 0, 0), unroll=4)

        def stream(a, t, y):
            c = PIECE[2 * y]
            u = lax.rem(me, 4)
            j = lax.rem(2 * u + t, half)
            return [pltpu.make_async_remote_copy(
                src_ref=packs[a].at[pl.ds(j * c, c)], dst_ref=land[a][2 * y + core].at[pl.ds(c, c)], send_sem=st_send.at[a, t], recv_sem=st_recv.at[a, 2 * y + core],
                device_id={"cp": other + j}, device_id_type=MESH) for core in range(2)]

        def streams(act):
            for y in range(2):
                for core in range(2):
                    @pl.when(inner & (lax.rem(me, 4) == 2 * y + core))
                    def _():
                        for a in range(2):
                            for t in range(half):
                                act(stream(a, t, y)[core])

        streams(start)
        for to, ok in zip(near, apart):
            @pl.when(inner & ok)
            def _():
                both(to, start)

    pos = [lens_ref[me * rows + b] for b in range(rows)]

    for name in ("freq", "x", "gain", "bq", "bk", "bv", "wk", "wv", "wq"):
        loads[name].wait()
    wide = xs[...].astype(F32)
    inv = lax.rsqrt(jnp.mean(wide * wide, axis=-1, keepdims=True) + RMS_EPS)
    gains = jnp.concatenate([gain[i:i + 1, :].astype(F32) for i in range(heads)], axis=1)
    normed = (wide * inv * gains).astype(BF16)
    which = lax.broadcasted_iota(jnp.int32, (rows, dim), 0)
    lane = lax.broadcasted_iota(jnp.int32, (rows, dim), 1)
    posf = jnp.zeros((rows, dim), F32)
    for b in range(rows):
        posf = jnp.where(which == b, pos[b].astype(F32), posf)
    angle = posf * freq_ref[...]
    cos_t = jnp.cos(angle)
    sin_t = jnp.sin(angle)
    sin_t = jnp.where(lane < dim // 2, -sin_t, sin_t)

    def rotate(t):
        return (t * cos_t + pltpu.roll(t, dim // 2, 1) * sin_t).astype(BF16).astype(F32)

    for i in range(2):
        cols = pl.ds(i * dim, dim)
        kn_s[:, i, :] = rotate(jnp.dot(normed, wk[:, cols], preferred_element_type=F32) + bk[i:i + 1, :].astype(F32))
        vn_s[:, i, :] = (jnp.dot(normed, wv[:, cols], preferred_element_type=F32) + bv[i:i + 1, :].astype(F32)).astype(BF16).astype(F32)
    for i in range(heads):
        q_s[:, i, :] = rotate(jnp.dot(normed, wq[:, i * dim:(i + 1) * dim], preferred_element_type=F32) + bq[i:i + 1, :].astype(F32))

    row = lax.broadcasted_iota(jnp.int32, (m, dim), 0)
    even = lax.rem(row, 2) == 0

    def merge(raw, new, out, b, i):
        at = 2 * pos[b] - i * m
        fresh = jnp.where(even, new[b, 0:1, :], new[b, 1:2, :])
        merged = jnp.where(row < at, raw.astype(F32), jnp.where(row < at + 2, fresh, 0.0)).astype(BF16)
        out[b, i] = merged
        return merged

    def k_block(i, get):
        cols = pl.ds(pl.multiple_of(i * m, m), m)
        for b in range(rows):
            keys = merge(get(b), kn_s, ko_ref, b, i)
            s_s[b, :, cols] = lax.dot_general(q_s[b].astype(BF16), keys, (((1,), (1,)), ((), ())), preferred_element_type=F32) * (dim ** -0.5)

    def v_block(i, get):
        cols = pl.ds(pl.multiple_of(i * m, m), m)
        for b in range(rows):
            vals = merge(get(b), vn_s, vo_ref, b, i)
            acc[b] += jnp.dot(e_s[b, :, cols], vals, preferred_element_type=F32)

    def direct(a, block):
        def visit(d, c):
            src = lax.rem(me + n - d, n)

            def go():
                arrive(a, src)
                block(src, lambda b: pairs[a][1][b, src])

            if pooled:
                pl.when((lax.div(src, half) == high) | (lax.rem(lax.div(src, 4) + lax.div(src, half), 2) == 0))(go)
            else:
                go()
            return c

        lax.fori_loop(1, n, visit, 0)

    def pooled_blocks(a, block):
        for u in range(4):
            c = PIECE[u]
            for side in range(2):
                @pl.when(h > 0 if side == 0 else h < half - 1)
                def _():
                    forward(a, u, 1 - side).wait_recv()
        for u in range(4):
            c = PIECE[u]
            i = half - 4 * high + u

            def get(b):
                loc = place_s[u, h * rows + b] - (h - 1) * c
                return land[a][u][jnp.clip(loc, 0, 3 * c - 1)]

            block(i, get)

    def forward(a, u, side):
        c = PIECE[u]
        to = high * half + lax.rem(h + (1 if side else half - 1), half)
        return pltpu.make_async_remote_copy(
            src_ref=land[a][u].at[pl.ds(c, c)], dst_ref=land[a][u].at[pl.ds(0 if side else 2 * c, c)], send_sem=fw_send.at[a, u, side], recv_sem=fw_recv.at[a, u, side],
            device_id={"cp": to}, device_id_type=MESH)

    def forwards(a, u, act):
        @pl.when(h < half - 1)
        def _():
            act(forward(a, u, 1))

        @pl.when(h > 0)
        def _():
            act(forward(a, u, 0))

    if pooled:
        for a in range(2):
            for u in range(4):
                c = PIECE[u]
                pltpu.make_async_remote_copy(
                    src_ref=packs[a].at[pl.ds(0, c)], dst_ref=land[a][u].at[pl.ds(c, c)], send_sem=st_send.at[a, 0], recv_sem=st_recv.at[a, u],
                    device_id={"cp": me}, device_id_type=MESH).wait_recv()
                forwards(a, u, start)

        @pl.when(outer)
        def _():
            send(1, far[0]).start()
            for to in far[1:]:
                both(to, start)

    loads["k"].wait()
    k_block(me, lambda b: k_land[b, me])
    direct(0, k_block)
    if pooled:
        pooled_blocks(0, k_block)

    col = lax.broadcasted_iota(jnp.int32, (heads, n * m), 1)
    head = lax.broadcasted_iota(jnp.int32, (heads, n * m), 0)
    own = lax.rem(col, 2) == lax.div(head, heads // 2)
    for b in range(rows):
        valid = own & (col < 2 * pos[b] + 2)
        s = jnp.where(valid, s_s[b], -1e30)
        e = jnp.where(valid, jnp.exp(s - jnp.max(s, axis=-1, keepdims=True)), 0.0)
        l_s[b] = jnp.broadcast_to(jnp.sum(e, axis=-1, keepdims=True), (heads, dim))
        e_s[b] = e.astype(BF16)
    acc[...] = jnp.zeros_like(acc)

    loads["v"].wait()
    v_block(me, lambda b: v_land[b, me])
    loads["wo"].wait()
    if pooled:
        pooled_blocks(1, v_block)
    direct(1, v_block)

    acc[...] = acc[...] / l_s[...]
    att_ref[...] = jnp.concatenate([acc[:, i, :] for i in range(heads)], axis=1).astype(BF16)

    if not pooled:
        for d in range(1, n):
            both(lax.rem(me + d, n), sent)
    else:
        for to in near:
            both(to, sent)

        @pl.when(outer)
        def _():
            for to in far:
                both(to, sent)

        streams(sent)
        for a in range(2):
            for u in range(4):
                forwards(a, u, sent)


def step(pooled, lens, freq, x, gain, b_q, b_k, b_v, w_q, w_k, w_v, w_o, k, v):
    n, rows, m, dim = k.shape
    heads = w_q.shape[1] // dim
    kv = w_k.shape[1] // dim
    half = n // 2
    cache = pltpu.VMEM((rows, n, m, dim), BF16)
    hbm = pl.BlockSpec(memory_space=pltpu.HBM)
    vmem = pl.BlockSpec(memory_space=pltpu.VMEM)
    dma = pltpu.SemaphoreType.DMA
    scratch = [
        pltpu.SMEM(lens.shape, jnp.int32), pltpu.VMEM(freq.shape, F32),
        pltpu.VMEM((rows, n, m, dim), BF16), pltpu.VMEM((rows, n, m, dim), BF16),
        pltpu.VMEM(w_q.shape, BF16), pltpu.VMEM(w_k.shape, BF16), pltpu.VMEM(w_v.shape, BF16),
        pltpu.VMEM(x.shape, BF16), pltpu.VMEM(gain.shape, BF16), pltpu.VMEM(b_q.shape, BF16), pltpu.VMEM(b_k.shape, BF16), pltpu.VMEM(b_v.shape, BF16),
        pltpu.VMEM((rows, heads, dim), F32), pltpu.VMEM((rows, kv, dim), F32), pltpu.VMEM((rows, kv, dim), F32),
        pltpu.VMEM((rows, heads, n * m), F32), pltpu.VMEM((rows, heads, n * m), BF16), pltpu.VMEM((rows, heads, dim), F32),
        pltpu.VMEM((rows, heads, dim), F32),
        dma((2, n)), dma((2, n)), dma((13,))]
    if pooled:
        scratch += [pltpu.VMEM((half * rows, m, dim), BF16)] * 2 + [pltpu.VMEM((half * max(PIECE), m, dim), BF16)] * 2
        scratch += [pltpu.SMEM((half * rows + 1,), jnp.int32), pltpu.SMEM((half * max(PIECE),), jnp.int32), pltpu.SMEM((4, half * rows), jnp.int32)]
        scratch += [dma((2, half)), dma((2, half)), dma((2, 4)), dma((2, 4, 2)), dma((2, 4, 2))]
        scratch += [pltpu.VMEM((3 * c, m, dim), BF16) for _ in range(2) for c in PIECE]
    return pl.pallas_call(
        functools.partial(step_kernel, n, pooled),
        out_shape=[pltpu.VMEM(x.shape, BF16), cache, cache, pltpu.VMEM(w_o.shape, BF16)],
        in_specs=[hbm] * 13,
        out_specs=[vmem] * 4,
        scratch_shapes=scratch,
        compiler_params=pltpu.CompilerParams(collective_id=int(pooled), has_side_effects=True, vmem_limit_bytes=47 * 1024 * 1024),
    )(lens, freq, x, gain, b_q, b_k, b_v, w_q, w_k, w_v, w_o, k, v)


def fits(lens, n, rows, slots):
    half = n // 2
    c = np.array(PIECE * 2)[:, None, None]
    src = np.arange(n // 4, n - n // 4)
    k, j = np.arange(half)[None, :, None], np.arange(half)[None, None, :]
    room = np.minimum((j + 2) * c, half * c) - np.maximum(k - 1, 0) * c
    room = np.where(k <= j, room, n * rows)
    owner = np.arange(half * rows) // rows
    between = (owner >= np.arange(half)[:, None, None]) & (owner <= np.arange(half)[None, :, None])
    seqs = jnp.concatenate([jnp.broadcast_to(lens[half * rows:], (half // 2, half * rows)), jnp.broadcast_to(lens[:half * rows], (half // 2, half * rows))])
    need = (seqs > jnp.asarray(src * slots)[:, None]).astype(F32)
    used = jnp.dot(need, jnp.asarray(between.reshape(half * half, -1).T.astype(np.float32)))
    return jnp.all(used <= jnp.asarray(room.reshape(half, -1).astype(np.float32)))


def finish_kernel(x_ref, att_ref, wo_ref, k_ref, v_ref, y_ref, ko_ref, vo_ref, sem):
    copies = [pltpu.make_async_copy(k_ref, ko_ref, sem.at[0]), pltpu.make_async_copy(v_ref, vo_ref, sem.at[1])]
    for copy in copies:
        copy.start()
    tile = 256
    for t in range(wo_ref.shape[1] // tile):
        cols = slice(t * tile, (t + 1) * tile)
        y_ref[:, cols] = (x_ref[:, cols].astype(F32) + jnp.dot(att_ref[...], wo_ref[:, cols], preferred_element_type=F32)).astype(BF16)
    for copy in copies:
        copy.wait()


def finish(x, att, w_o, k, v):
    vmem = pl.BlockSpec(memory_space=pltpu.VMEM)
    hbm = pl.BlockSpec(memory_space=pltpu.HBM)
    cache = jax.ShapeDtypeStruct(k.shape, BF16)
    return pl.pallas_call(
        finish_kernel,
        out_shape=[jax.ShapeDtypeStruct(x.shape, BF16), cache, cache],
        in_specs=[vmem] * 5,
        out_specs=[vmem, hbm, hbm],
        scratch_shapes=[pltpu.SemaphoreType.DMA((2,))],
        compiler_params=pltpu.CompilerParams(vmem_limit_bytes=4 * 1024 * 1024),
    )(x, att, w_o, k, v)


def solution(mesh):
    batch_spec = P(('dp', 'cp'))
    seq_spec = P('dp', 'cp')
    whole = P()

    def per_device(x_tok, prompt_lens, k_cache, v_cache, norm_gain, w_q, b_q, w_k, b_k, w_v, b_v, w_o):
        rows = x_tok.shape[0]
        batch, slots, kv_heads, dim = k_cache.shape
        n = batch // rows
        inv_freq = np.power(np.float32(ROPE_THETA), -(np.arange(dim // 2, dtype=np.float32) * 2.0 / dim)).astype(np.float32)
        freq = jnp.asarray(np.concatenate([inv_freq, inv_freq])[None, :])
        pack = (n, rows, slots * kv_heads, dim)
        args = (prompt_lens, freq, x_tok, norm_gain.reshape(-1, dim), b_q.reshape(-1, dim), b_k.reshape(-1, dim), b_v.reshape(-1, dim),
                w_q, w_k, w_v, w_o, k_cache.reshape(pack), v_cache.reshape(pack))

        def run(pooled, *args):
            att, k_all, v_all, wo = step(pooled, *args)
            return finish(x_tok, att, wo, k_all, v_all)

        y_out, k_out, v_out = lax.cond(fits(prompt_lens, n, rows, slots), functools.partial(run, True), functools.partial(run, False), *args)
        shape = (rows, n * slots, kv_heads, dim)
        return y_out, k_out.reshape(shape), v_out.reshape(shape)

    return jax.shard_map(per_device, mesh=mesh, in_specs=(batch_spec, P('dp'), seq_spec, seq_spec, whole, whole, whole, whole, whole, whole, whole, whole), out_specs=(batch_spec, batch_spec, batch_spec), check_vma=False)
```

time: 193 us -> 239 us (1.24)
  the two profiles are of different devices: /device:TPU:29 before, /device:TPU:16 now
where the time goes in v8:
time: 239 us
  Pallas kernels  235 us (98%)
    pallas_call x1, Pallas kernels, step(): pl.pallas_call(functools.partial(step_kernel, n, pooled), out_shape=[pltp...  231 us

profile of v8, /device:TPU:16, one launch (start us, length us, event | category | flops | bytes accessed | tf_op | source)
XLA Modules:
  0.0 238.8 jit_solution(4788050578850834196)
XLA Ops:
  0.6 0.8 fusion.3
  1.4 1.5 fusion
  3.6 234.9 %conditional.1 = ((bf16[8,2048]{1,0:T(8,128)(2,1)}, bf16[8,16,128,128]{3,2,1,0:T(8,128)(2,1)}, bf16[8,16,128,128]{3,2,1,0:T(8,128)(2,1)})) conditional(s32[]{:T(128)} %convert_element_type.4, (s32[128]{0:T(128)}, f32[1,128]{1,0:T(1,128)}, bf16[8,2048]{1,0:T(8,128)(2,1)}, bf16[16,128]{1,0:T(8,128)(2,1)}, bf16[16,128]{1,0:T(8,128)(2,1)}, ...), branch_computations={%region_1.0_spmd.clone, %region_2.0_spmd.clone} | conditional | bytes 131108 | solution.py:430
  3.7 0.0 copy-start.1
  3.7 230.6 %branch_1_fun.2 = (bf16[8,2048]{1,0:T(8,128)(2,1)S(1)}, bf16[8,16,128,128]{3,2,1,0:T(8,128)(2,1)S(1)}, bf16[8,16,128,128]{3,2,1,0:T(8,128)(2,1)S(1)}, bf16[2048,2048]{1,0:T(8,128)(2,1)S(1)}) custom-call(s32[128]{0:T(128)} %get-tuple-element.127.lens_hbm, f32[1,128]{1,0:T(1,128)} %get-tuple-element.128.freq_hbm, bf16[8,2048]{1,0:T(8,128)(2,1)} %get-tuple-element.126.x_ref, ...), custom_call_target="tpu_custom_call" | custom-call | tf_op jit(solution)/shard_map/cond/branch_1_fun/pallas_call | solution.py:360
  234.3 0.0 copy-done.1
  234.3 4.1 %branch_1_fun.3 = (bf16[8,2048]{1,0:T(8,128)(2,1)}, bf16[8,16,128,128]{3,2,1,0:T(8,128)(2,1)}, bf16[8,16,128,128]{3,2,1,0:T(8,128)(2,1)}) custom-call(bf16[8,2048]{1,0:T(8,128)(2,1)S(1)} %copy-done.1, bf16[8,2048]{1,0:T(8,128)(2,1)S(1)} %get-tuple-element.139.att_ref, bf16[2048,2048]{1,0:T(8,128)(2,1)S(1)} %get-tuple-element.140.wo_ref, ...), custom_call_target="tpu_custom_call" | custom-call | tf_op jit(solution)/shard_map/cond/branch_1_fun/pallas_call | solution.py:401
  (2 shorter events, 0.0 us)
Async XLA Ops:
  3.7 230.6 %copy-start.1 = (bf16[8,2048]{1,0:T(8,128)(2,1)S(1)}, bf16[8,2048]{1,0:T(8,128)(2,1)}, u32[]{:S(2)}) copy-start(bf16[8,2048]{1,0:T(8,128)(2,1)} %get-tuple-element.126.x_ref) | copy-start | bytes 98308 | tf_op jit(solution)/shard_map/cond

commit v9 on v8

--- a/solution.py
+++ b/solution.py
@@ -72,7 +72,7 @@
         pl.semaphore_signal(barrier, inc=1, device_id={"cp": lax.rem(me + d, n)}, device_id_type=MESH)
     loads["lens"].start()
     if pooled:
-        (k_all, v_all, k_pack, v_pack, next_s, pick_s, place_s, gather_sem, st_send, st_recv, fw_send, fw_recv), land = pool[:12], (pool[12:16], pool[16:20])
+        (k_all, v_all, k_pack, v_pack, next_s, pick_s, place_s, gather_sem, st_send, st_recv, fw_send, fw_recv, gate), land = pool[:13], (pool[13:17], pool[17:21])
         caches, packs = (k_all, v_all), (k_pack, v_pack)
 
         def gather(a, j):
@@ -283,8 +283,16 @@
                     device_id={"cp": me}, device_id_type=MESH).wait_recv()
                 forwards(a, u, start)
 
+        streams(sent)
+
+        @pl.when(inner)
+        def _():
+            for u in range(4):
+                pl.semaphore_signal(gate, inc=1, device_id={"cp": 3 * half * high // 2 + u}, device_id_type=MESH)
+
         @pl.when(outer)
         def _():
+            pl.semaphore_wait(gate, 4)
             send(1, far[0]).start()
             for to in far[1:]:
                 both(to, start)
@@ -328,7 +336,6 @@
             for to in far:
                 both(to, sent)
 
-        streams(sent)
         for a in range(2):
             for u in range(4):
                 forwards(a, u, sent)
@@ -355,7 +362,7 @@
     if pooled:
         scratch += [pltpu.VMEM((half * rows, m, dim), BF16)] * 2 + [pltpu.VMEM((half * max(PIECE), m, dim), BF16)] * 2
         scratch += [pltpu.SMEM((half * rows + 1,), jnp.int32), pltpu.SMEM((half * max(PIECE),), jnp.int32), pltpu.SMEM((4, half * rows), jnp.int32)]
-        scratch += [dma((2, half)), dma((2, half)), dma((2, 4)), dma((2, 4, 2)), dma((2, 4, 2))]
+        scratch += [dma((2, half)), dma((2, half)), dma((2, 4)), dma((2, 4, 2)), dma((2, 4, 2)), pltpu.SemaphoreType.REGULAR]
         scratch += [pltpu.VMEM((3 * c, m, dim), BF16) for _ in range(2) for c in PIECE]
     return pl.pallas_call(
         functools.partial(step_kernel, n, pooled),

time: 239 us -> 197 us (0.82)
  the two profiles are of different devices: /device:TPU:16 before, /device:TPU:0 now
where the time goes in v9:
time: 197 us; the launch traced here: 194 us
  Pallas kernels  190 us (96%)
    pallas_call x1, Pallas kernels, step(): pl.pallas_call(functools.partial(step_kernel, n, pooled), out_shape=[pltp...  186 us
    pallas_call x1, Pallas kernels, finish(): pl.pallas_call(finish_kernel, out_shape=[jax.ShapeDtypeStruct(x.shape, BF...  4.07 us

profile of v9, /device:TPU:0, one launch (start us, length us, event | category | flops | bytes accessed | tf_op | source)
XLA Modules:
  0.0 194.3 jit_solution(6964748636194703889)
XLA Ops:
  0.6 0.8 fusion.3
  1.4 1.5 fusion
  3.6 190.5 %conditional.1 = ((bf16[8,2048]{1,0:T(8,128)(2,1)}, bf16[8,16,128,128]{3,2,1,0:T(8,128)(2,1)}, bf16[8,16,128,128]{3,2,1,0:T(8,128)(2,1)})) conditional(s32[]{:T(128)} %convert_element_type.4, (s32[128]{0:T(128)}, f32[1,128]{1,0:T(1,128)}, bf16[8,2048]{1,0:T(8,128)(2,1)}, bf16[16,128]{1,0:T(8,128)(2,1)}, bf16[16,128]{1,0:T(8,128)(2,1)}, ...), branch_computations={%region_1.0_spmd.clone, %region_2.0_spmd.clone} | conditional | bytes 131108 | solution.py:437
  3.7 0.0 copy-start.1
  3.7 186.1 %branch_1_fun.2 = (bf16[8,2048]{1,0:T(8,128)(2,1)S(1)}, bf16[8,16,128,128]{3,2,1,0:T(8,128)(2,1)S(1)}, bf16[8,16,128,128]{3,2,1,0:T(8,128)(2,1)S(1)}, bf16[2048,2048]{1,0:T(8,128)(2,1)S(1)}) custom-call(s32[128]{0:T(128)} %get-tuple-element.127.lens_hbm, f32[1,128]{1,0:T(1,128)} %get-tuple-element.128.freq_hbm, bf16[8,2048]{1,0:T(8,128)(2,1)} %get-tuple-element.126.x_ref, ...), custom_call_target="tpu_custom_call" | custom-call | tf_op jit(solution)/shard_map/cond/branch_1_fun/pallas_call | solution.py:367
  189.8 0.0 copy-done.1
  189.8 4.1 %branch_1_fun.3 = (bf16[8,2048]{1,0:T(8,128)(2,1)}, bf16[8,16,128,128]{3,2,1,0:T(8,128)(2,1)}, bf16[8,16,128,128]{3,2,1,0:T(8,128)(2,1)}) custom-call(bf16[8,2048]{1,0:T(8,128)(2,1)S(1)} %copy-done.1, bf16[8,2048]{1,0:T(8,128)(2,1)S(1)} %get-tuple-element.139.att_ref, bf16[2048,2048]{1,0:T(8,128)(2,1)S(1)} %get-tuple-element.140.wo_ref, ...), custom_call_target="tpu_custom_call" | custom-call | tf_op jit(solution)/shard_map/cond/branch_1_fun/pallas_call | solution.py:408
  (2 shorter events, 0.0 us)
Async XLA Ops:
  3.7 186.1 %copy-start.1 = (bf16[8,2048]{1,0:T(8,128)(2,1)S(1)}, bf16[8,2048]{1,0:T(8,128)(2,1)}, u32[]{:S(2)}) copy-start(bf16[8,2048]{1,0:T(8,128)(2,1)} %get-tuple-element.126.x_ref) | copy-start | bytes 98308 | tf_op jit(solution)/shard_map/cond

commit v10 on v8

--- a/solution.py
+++ b/solution.py
@@ -96,16 +96,14 @@
     else:
         near = [high * half + lax.rem(h + t, half) for t in range(1, half)]
         far = [other + lax.rem(h + t, half) for t in range(half)]
-        beside = [lax.div(to, 4) == lax.div(me, 4) for to in near]
-        apart = [lax.div(to, 4) != lax.div(me, 4) for to in near]
-        for to, ok in zip(near, beside):
-            @pl.when(outer | ok)
-            def _():
+
+        @pl.when(outer)
+        def _():
+            for to in far:
                 both(to, start)
 
-        @pl.when(outer)
-        def _():
-            send(0, far[0]).start()
+        for to in near:
+            both(to, start)
 
         loads["lens"].wait()
         mine = jnp.where(lax.rem(me, 4) < 2, PIECE[0], PIECE[2])
@@ -170,10 +168,6 @@
                                 act(stream(a, t, y)[core])
 
         streams(start)
-        for to, ok in zip(near, apart):
-            @pl.when(inner & ok)
-            def _():
-                both(to, start)
 
     pos = [lens_ref[me * rows + b] for b in range(rows)]
 
@@ -274,25 +268,22 @@
         def _():
             act(forward(a, u, 0))
 
-    if pooled:
-        for a in range(2):
+    def relay(a):
+        for r in range(4):
             for u in range(4):
-                c = PIECE[u]
-                pltpu.make_async_remote_copy(
-                    src_ref=packs[a].at[pl.ds(0, c)], dst_ref=land[a][u].at[pl.ds(c, c)], send_sem=st_send.at[a, 0], recv_sem=st_recv.at[a, u],
-                    device_id={"cp": me}, device_id_type=MESH).wait_recv()
-                forwards(a, u, start)
-
-        @pl.when(outer)
-        def _():
-            send(1, far[0]).start()
-            for to in far[1:]:
-                both(to, start)
+                @pl.when(lax.rem(lax.div(h, 2) + 4 - r, 4) == u)
+                def _():
+                    c = PIECE[u]
+                    pltpu.make_async_remote_copy(
+                        src_ref=packs[a].at[pl.ds(0, c)], dst_ref=land[a][u].at[pl.ds(c, c)], send_sem=st_send.at[a, 0], recv_sem=st_recv.at[a, u],
+                        device_id={"cp": me}, device_id_type=MESH).wait_recv()
+                    forwards(a, u, start)
 
     loads["k"].wait()
     k_block(me, lambda b: k_land[b, me])
     direct(0, k_block)
     if pooled:
+        relay(0)
         pooled_blocks(0, k_block)
 
     col = lax.broadcasted_iota(jnp.int32, (heads, n * m), 1)
@@ -309,9 +300,10 @@
     loads["v"].wait()
     v_block(me, lambda b: v_land[b, me])
     loads["wo"].wait()
+    direct(1, v_block)
     if pooled:
+        relay(1)
         pooled_blocks(1, v_block)
-    direct(1, v_block)
 
     acc[...] = acc[...] / l_s[...]
     att_ref[...] = jnp.concatenate([acc[:, i, :] for i in range(heads)], axis=1).astype(BF16)

time: 239 us -> 205 us (0.86)
  the two profiles are of different devices: /device:TPU:16 before, /device:TPU:19 now
where the time goes in v10:
time: 205 us
  Pallas kernels  201 us (98%)
    pallas_call x1, Pallas kernels, step(): pl.pallas_call(functools.partial(step_kernel, n, pooled), out_shape=[pltp...  196 us

profile of v10, /device:TPU:19, one launch (start us, length us, event | category | flops | bytes accessed | tf_op | source)
XLA Modules:
  0.0 204.6 jit_solution(12312588972042127145)
XLA Ops:
  0.6 0.8 fusion.3
  1.4 1.5 fusion
  3.6 200.8 %conditional.1 = ((bf16[8,2048]{1,0:T(8,128)(2,1)}, bf16[8,16,128,128]{3,2,1,0:T(8,128)(2,1)}, bf16[8,16,128,128]{3,2,1,0:T(8,128)(2,1)})) conditional(s32[]{:T(128)} %convert_element_type.4, (s32[128]{0:T(128)}, f32[1,128]{1,0:T(1,128)}, bf16[8,2048]{1,0:T(8,128)(2,1)}, bf16[16,128]{1,0:T(8,128)(2,1)}, bf16[16,128]{1,0:T(8,128)(2,1)}, ...), branch_computations={%region_1.0_spmd.clone, %region_2.0_spmd.clone} | conditional | bytes 131108 | solution.py:422
  3.7 0.0 copy-start.1
  3.7 196.5 %branch_1_fun.2 = (bf16[8,2048]{1,0:T(8,128)(2,1)S(1)}, bf16[8,16,128,128]{3,2,1,0:T(8,128)(2,1)S(1)}, bf16[8,16,128,128]{3,2,1,0:T(8,128)(2,1)S(1)}, bf16[2048,2048]{1,0:T(8,128)(2,1)S(1)}) custom-call(s32[128]{0:T(128)} %get-tuple-element.127.lens_hbm, f32[1,128]{1,0:T(1,128)} %get-tuple-element.128.freq_hbm, bf16[8,2048]{1,0:T(8,128)(2,1)} %get-tuple-element.126.x_ref, ...), custom_call_target="tpu_custom_call" | custom-call | tf_op jit(solution)/shard_map/cond/branch_1_fun/pallas_call | solution.py:352
  200.1 0.0 copy-done.1
  200.2 4.1 %branch_1_fun.3 = (bf16[8,2048]{1,0:T(8,128)(2,1)}, bf16[8,16,128,128]{3,2,1,0:T(8,128)(2,1)}, bf16[8,16,128,128]{3,2,1,0:T(8,128)(2,1)}) custom-call(bf16[8,2048]{1,0:T(8,128)(2,1)S(1)} %copy-done.1, bf16[8,2048]{1,0:T(8,128)(2,1)S(1)} %get-tuple-element.139.att_ref, bf16[2048,2048]{1,0:T(8,128)(2,1)S(1)} %get-tuple-element.140.wo_ref, ...), custom_call_target="tpu_custom_call" | custom-call | tf_op jit(solution)/shard_map/cond/branch_1_fun/pallas_call | solution.py:393
  (2 shorter events, 0.0 us)
Async XLA Ops:
  3.7 196.5 %copy-start.1 = (bf16[8,2048]{1,0:T(8,128)(2,1)S(1)}, bf16[8,2048]{1,0:T(8,128)(2,1)}, u32[]{:S(2)}) copy-start(bf16[8,2048]{1,0:T(8,128)(2,1)} %get-tuple-element.126.x_ref) | copy-start | bytes 98308 | tf_op jit(solution)/shard_map/cond

commit v11 on v7

--- a/solution.py
+++ b/solution.py
@@ -25,7 +25,7 @@
 def step_kernel(n, lens_hbm, freq_hbm, x_ref, gain_ref, bq_ref, bk_ref, bv_ref, wq_ref, wk_ref, wv_ref, wo_ref, k_ref, v_ref,
                 att_ref, ko_ref, vo_ref, wo,
                 lens_ref, freq_ref, k_land, v_land, wq, wk, wv, xs, gain, bq, bk, bv,
-                q_s, kn_s, vn_s, s_s, e_s, l_s, acc, send_sem, recv_sem, load_sem):
+                q_s, kn_s, vn_s, s_s, e_s, l_s, acc, send_sem, recv_sem, load_sem, turn):
     me = lax.axis_index("cp")
     rows, heads, dim = q_s.shape
     m = k_land.shape[2]
@@ -46,22 +46,49 @@
 
     pairs = ((k_ref, k_land), (v_ref, v_land))
 
-    def send(a, d):
-        to = lax.rem(me + d, n)
+    def send(a, to):
         return pltpu.make_async_remote_copy(
-            src_ref=pairs[a][0].at[to], dst_ref=pairs[a][1].at[:, me], send_sem=send_sem.at[a, d], recv_sem=recv_sem.at[a, me],
+            src_ref=pairs[a][0].at[to], dst_ref=pairs[a][1].at[:, me], send_sem=send_sem.at[a, to], recv_sem=recv_sem.at[a, me],
             device_id={"cp": to}, device_id_type=MESH)
 
     def arrive(a, d):
         src = lax.rem(me + n - d, n)
         pltpu.make_async_remote_copy(
-            src_ref=pairs[a][0].at[0], dst_ref=pairs[a][1].at[:, src], send_sem=send_sem.at[a, d], recv_sem=recv_sem.at[a, src],
+            src_ref=pairs[a][0].at[0], dst_ref=pairs[a][1].at[:, src], send_sem=send_sem.at[a, src], recv_sem=recv_sem.at[a, src],
             device_id={"cp": src}, device_id_type=MESH).wait_recv()
         return src
 
-    plan = [(a, d) for d in range(1, n) for a in range(2)]
-    for a, d in plan:
-        send(a, d).start()
+    half, layer = n // 2, n // 4
+    z = lax.div(me, layer)
+    high = lax.div(me, half)
+    end = lax.rem(z + high, 2) == 0
+    middle = lax.rem(z + high, 2) == 1
+    second = lax.rem(me, 2) == 1
+    beside = [z * layer + lax.rem(me + t, layer) for t in range(1, layer)]
+    near = [(4 * high + 1 - z) * layer + lax.rem(me + t, layer) for t in range(layer)]
+    far = [(1 - high) * half + lax.rem(me + t, half) for t in range(half)]
+
+    def each(targets, act):
+        for to in targets:
+            for a in range(2):
+                act(send(a, to))
+
+    def start(copy):
+        copy.start()
+
+    def sent(copy):
+        copy.wait_send()
+
+    each(beside, start)
+
+    def along():
+        pl.when(end)(lambda: each(near, start))
+        each(far, start)
+        pl.when(middle)(lambda: each(near, start))
+
+    @pl.when(middle | (lax.rem(me, 2) == 0))
+    def _():
+        along()
 
     loads["lens"].wait()
     pos = [lens_ref[me * rows + b] for b in range(rows)]
@@ -92,6 +119,16 @@
     for h in range(heads):
         q_s[:, h, :] = rotate(jnp.dot(normed, wq[:, h * dim:(h + 1) * dim], preferred_element_type=F32) + bq[h:h + 1, :].astype(F32))
 
+    @pl.when(end & (lax.rem(me, 2) == 0))
+    def _():
+        each(near + far[:-1], sent)
+        pl.semaphore_signal(turn, inc=1, device_id={"cp": me + 1}, device_id_type=MESH)
+
+    @pl.when(end & second)
+    def _():
+        pl.semaphore_wait(turn, 1)
+        along()
+
     row = lax.broadcasted_iota(jnp.int32, (m, dim), 0)
     even = lax.rem(row, 2) == 0
 
@@ -145,8 +182,11 @@
     acc[...] = acc[...] / l_s[...]
     att_ref[...] = jnp.concatenate([acc[:, h, :] for h in range(heads)], axis=1).astype(BF16)
 
-    for a, d in plan:
-        send(a, d).wait_send()
+    each(beside + far[-1:], sent)
+
+    @pl.when(middle | second)
+    def _():
+        each(near + far[:-1], sent)
 
 
 def step(lens, freq, x, gain, b_q, b_k, b_v, w_q, w_k, w_v, w_o, k, v):
@@ -169,7 +209,7 @@
             pltpu.VMEM((rows, heads, dim), F32), pltpu.VMEM((rows, kv, dim), F32), pltpu.VMEM((rows, kv, dim), F32),
             pltpu.VMEM((rows, heads, n * m), F32), pltpu.VMEM((rows, heads, n * m), BF16), pltpu.VMEM((rows, heads, dim), F32),
             pltpu.VMEM((rows, heads, dim), F32),
-            pltpu.SemaphoreType.DMA((2, n)), pltpu.SemaphoreType.DMA((2, n)), pltpu.SemaphoreType.DMA((13,))],
+            pltpu.SemaphoreType.DMA((2, n)), pltpu.SemaphoreType.DMA((2, n)), pltpu.SemaphoreType.DMA((13,)), pltpu.SemaphoreType.REGULAR],
         compiler_params=pltpu.CompilerParams(collective_id=0, has_side_effects=True, vmem_limit_bytes=47 * 1024 * 1024),
     )(lens, freq, x, gain, b_q, b_k, b_v, w_q, w_k, w_v, w_o, k, v)
 

time: 193 us -> 204 us (1.057)
  the two profiles are of different devices: /device:TPU:29 before, /device:TPU:0 now
where the time goes in v11:
time: 204 us
  Pallas kernels  203 us (100%)
    pallas_call x1, Pallas kernels, step(): pl.pallas_call(functools.partial(step_kernel, n), out_shape=[pltpu.VMEM(x...  199 us

profile of v11, /device:TPU:0, one launch (start us, length us, event | category | flops | bytes accessed | tf_op | source)
XLA Modules:
  0.0 203.6 jit_solution(6949787593440493514)
XLA Ops:
  0.6 0.0 copy-start
  0.6 198.9 %shard_map.148 = (bf16[8,2048]{1,0:T(8,128)(2,1)S(1)}, bf16[8,16,128,128]{3,2,1,0:T(8,128)(2,1)S(1)}, bf16[8,16,128,128]{3,2,1,0:T(8,128)(2,1)S(1)}, bf16[2048,2048]{1,0:T(8,128)(2,1)S(1)}) custom-call(s32[128]{0:T(128)} %lens_hbm.1, f32[1,128]{1,0:T(1,128)} %constant.2.clone.freq_hbm, bf16[8,2048]{1,0:T(8,128)(2,1)} %x_ref.3, bf16[16,128]{1,0:T(8,128)(2,1)} %bitcast.10, ...), custom_call_target="tpu_custom_call" | custom-call | tf_op jit(solution)/shard_map/pallas_call | solution.py:199
  199.6 0.0 copy-done
  199.6 4.1 %shard_map.149 = (bf16[8,2048]{1,0:T(8,128)(2,1)}, bf16[8,16,128,128]{3,2,1,0:T(8,128)(2,1)}, bf16[8,16,128,128]{3,2,1,0:T(8,128)(2,1)}) custom-call(bf16[8,2048]{1,0:T(8,128)(2,1)S(1)} %copy-done, bf16[8,2048]{1,0:T(8,128)(2,1)S(1)} %get-tuple-element.10.att_ref, bf16[2048,2048]{1,0:T(8,128)(2,1)S(1)} %get-tuple-element.11.wo_ref, ...), custom_call_target="tpu_custom_call" | custom-call | tf_op jit(solution)/shard_map/pallas_call | solution.py:233
Async XLA Ops:
  0.6 198.9 %copy-start = (bf16[8,2048]{1,0:T(8,128)(2,1)S(1)}, bf16[8,2048]{1,0:T(8,128)(2,1)}, u32[]{:S(2)}) copy-start(bf16[8,2048]{1,0:T(8,128)(2,1)} %x_ref.3) | copy-start | bytes 98308

commit v12 on v11

--- a/solution.py
+++ b/solution.py
@@ -81,14 +81,11 @@
 
     each(beside, start)
 
-    def along():
-        pl.when(end)(lambda: each(near, start))
+    @pl.when(middle)
+    def _():
         each(far, start)
-        pl.when(middle)(lambda: each(near, start))
-
-    @pl.when(middle | (lax.rem(me, 2) == 0))
-    def _():
-        along()
+
+    each(near, start)
 
     loads["lens"].wait()
     pos = [lens_ref[me * rows + b] for b in range(rows)]
@@ -119,15 +116,22 @@
     for h in range(heads):
         q_s[:, h, :] = rotate(jnp.dot(normed, wq[:, h * dim:(h + 1) * dim], preferred_element_type=F32) + bq[h:h + 1, :].astype(F32))
 
+    @pl.when(middle)
+    def _():
+        each(far[:-1], sent)
+        pl.semaphore_signal(turn, inc=1, device_id={"cp": 3 * layer * high + lax.rem(me, layer) - lax.rem(me, 2)}, device_id_type=MESH)
+
     @pl.when(end & (lax.rem(me, 2) == 0))
     def _():
-        each(near + far[:-1], sent)
+        pl.semaphore_wait(turn, 2)
+        each(far, start)
+        each(far[:-1], sent)
         pl.semaphore_signal(turn, inc=1, device_id={"cp": me + 1}, device_id_type=MESH)
 
     @pl.when(end & second)
     def _():
         pl.semaphore_wait(turn, 1)
-        along()
+        each(far, start)
 
     row = lax.broadcasted_iota(jnp.int32, (m, dim), 0)
     even = lax.rem(row, 2) == 0
@@ -182,11 +186,11 @@
     acc[...] = acc[...] / l_s[...]
     att_ref[...] = jnp.concatenate([acc[:, h, :] for h in range(heads)], axis=1).astype(BF16)
 
-    each(beside + far[-1:], sent)
-
-    @pl.when(middle | second)
-    def _():
-        each(near + far[:-1], sent)
+    each(beside + near + far[-1:], sent)
+
+    @pl.when(end & second)
+    def _():
+        each(far[:-1], sent)
 
 
 def step(lens, freq, x, gain, b_q, b_k, b_v, w_q, w_k, w_v, w_o, k, v):

time: 204 us -> 205 us (level)
  the two profiles are of different devices: /device:TPU:0 before, /device:TPU:1 now
where the time goes in v12:
time: 205 us
  Pallas kernels  204 us (100%)
    pallas_call x1, Pallas kernels, step(): pl.pallas_call(functools.partial(step_kernel, n), out_shape=[pltpu.VMEM(x...  200 us

profile of v12, /device:TPU:1, one launch (start us, length us, event | category | flops | bytes accessed | tf_op | source)
XLA Modules:
  0.0 204.9 jit_solution(18228656492799305929)
XLA Ops:
  0.6 0.0 copy-start
  0.6 200.1 %shard_map.148 = (bf16[8,2048]{1,0:T(8,128)(2,1)S(1)}, bf16[8,16,128,128]{3,2,1,0:T(8,128)(2,1)S(1)}, bf16[8,16,128,128]{3,2,1,0:T(8,128)(2,1)S(1)}, bf16[2048,2048]{1,0:T(8,128)(2,1)S(1)}) custom-call(s32[128]{0:T(128)} %lens_hbm.1, f32[1,128]{1,0:T(1,128)} %constant.2.clone.freq_hbm, bf16[8,2048]{1,0:T(8,128)(2,1)} %x_ref.3, bf16[16,128]{1,0:T(8,128)(2,1)} %bitcast.10, ...), custom_call_target="tpu_custom_call" | custom-call | tf_op jit(solution)/shard_map/pallas_call | solution.py:203
  200.8 0.0 copy-done
  200.8 4.1 %shard_map.149 = (bf16[8,2048]{1,0:T(8,128)(2,1)}, bf16[8,16,128,128]{3,2,1,0:T(8,128)(2,1)}, bf16[8,16,128,128]{3,2,1,0:T(8,128)(2,1)}) custom-call(bf16[8,2048]{1,0:T(8,128)(2,1)S(1)} %copy-done, bf16[8,2048]{1,0:T(8,128)(2,1)S(1)} %get-tuple-element.10.att_ref, bf16[2048,2048]{1,0:T(8,128)(2,1)S(1)} %get-tuple-element.11.wo_ref, ...), custom_call_target="tpu_custom_call" | custom-call | tf_op jit(solution)/shard_map/pallas_call | solution.py:237
Async XLA Ops:
  0.6 200.2 %copy-start = (bf16[8,2048]{1,0:T(8,128)(2,1)S(1)}, bf16[8,2048]{1,0:T(8,128)(2,1)}, u32[]{:S(2)}) copy-start(bf16[8,2048]{1,0:T(8,128)(2,1)} %x_ref.3) | copy-start | bytes 98308

commit v13 on v12

--- a/solution.py
+++ b/solution.py
@@ -65,8 +65,8 @@
     middle = lax.rem(z + high, 2) == 1
     second = lax.rem(me, 2) == 1
     beside = [z * layer + lax.rem(me + t, layer) for t in range(1, layer)]
-    near = [(4 * high + 1 - z) * layer + lax.rem(me + t, layer) for t in range(layer)]
-    far = [(1 - high) * half + lax.rem(me + t, half) for t in range(half)]
+    near = [(4 * high + 1 - z) * layer + t for t in range(layer)]
+    far = [(1 - high) * half + t for t in range(half)]
 
     def each(targets, act):
         for to in targets:

time: 205 us -> 214 us (1.044)
  the two profiles are of different devices: /device:TPU:1 before, /device:TPU:29 now
where the time goes in v13:
time: 214 us
  Pallas kernels  213 us (100%)
    pallas_call x1, Pallas kernels, step(): pl.pallas_call(functools.partial(step_kernel, n), out_shape=[pltpu.VMEM(x...  209 us

profile of v13, /device:TPU:29, one launch (start us, length us, event | category | flops | bytes accessed | tf_op | source)
XLA Modules:
  0.0 213.8 jit_solution(9869929452885190124)
XLA Ops:
  0.6 0.0 copy-start
  0.6 209.1 %shard_map.148 = (bf16[8,2048]{1,0:T(8,128)(2,1)S(1)}, bf16[8,16,128,128]{3,2,1,0:T(8,128)(2,1)S(1)}, bf16[8,16,128,128]{3,2,1,0:T(8,128)(2,1)S(1)}, bf16[2048,2048]{1,0:T(8,128)(2,1)S(1)}) custom-call(s32[128]{0:T(128)} %lens_hbm.1, f32[1,128]{1,0:T(1,128)} %constant.2.clone.freq_hbm, bf16[8,2048]{1,0:T(8,128)(2,1)} %x_ref.3, bf16[16,128]{1,0:T(8,128)(2,1)} %bitcast.10, ...), custom_call_target="tpu_custom_call" | custom-call | tf_op jit(solution)/shard_map/pallas_call | solution.py:203
  209.7 0.0 copy-done
  209.8 4.1 %shard_map.149 = (bf16[8,2048]{1,0:T(8,128)(2,1)}, bf16[8,16,128,128]{3,2,1,0:T(8,128)(2,1)}, bf16[8,16,128,128]{3,2,1,0:T(8,128)(2,1)}) custom-call(bf16[8,2048]{1,0:T(8,128)(2,1)S(1)} %copy-done, bf16[8,2048]{1,0:T(8,128)(2,1)S(1)} %get-tuple-element.10.att_ref, bf16[2048,2048]{1,0:T(8,128)(2,1)S(1)} %get-tuple-element.11.wo_ref, ...), custom_call_target="tpu_custom_call" | custom-call | tf_op jit(solution)/shard_map/pallas_call | solution.py:237
Async XLA Ops:
  0.6 209.1 %copy-start = (bf16[8,2048]{1,0:T(8,128)(2,1)S(1)}, bf16[8,2048]{1,0:T(8,128)(2,1)}, u32[]{:S(2)}) copy-start(bf16[8,2048]{1,0:T(8,128)(2,1)} %x_ref.3) | copy-start | bytes 98308

commit v14 on v13

--- a/solution.py
+++ b/solution.py
@@ -25,7 +25,7 @@
 def step_kernel(n, lens_hbm, freq_hbm, x_ref, gain_ref, bq_ref, bk_ref, bv_ref, wq_ref, wk_ref, wv_ref, wo_ref, k_ref, v_ref,
                 att_ref, ko_ref, vo_ref, wo,
                 lens_ref, freq_ref, k_land, v_land, wq, wk, wv, xs, gain, bq, bk, bv,
-                q_s, kn_s, vn_s, s_s, e_s, l_s, acc, send_sem, recv_sem, load_sem, turn):
+                q_s, kn_s, vn_s, s_s, e_s, l_s, acc, send_sem, recv_sem, load_sem):
     me = lax.axis_index("cp")
     rows, heads, dim = q_s.shape
     m = k_land.shape[2]
@@ -63,7 +63,6 @@
     high = lax.div(me, half)
     end = lax.rem(z + high, 2) == 0
     middle = lax.rem(z + high, 2) == 1
-    second = lax.rem(me, 2) == 1
     beside = [z * layer + lax.rem(me + t, layer) for t in range(1, layer)]
     near = [(4 * high + 1 - z) * layer + t for t in range(layer)]
     far = [(1 - high) * half + t for t in range(half)]
@@ -79,13 +78,13 @@
     def sent(copy):
         copy.wait_send()
 
-    each(beside, start)
-
     @pl.when(middle)
     def _():
-        each(far, start)
-
-    each(near, start)
+        each(far[:6] + beside + near + far[6:], start)
+
+    @pl.when(end)
+    def _():
+        each(beside + near + far, start)
 
     loads["lens"].wait()
     pos = [lens_ref[me * rows + b] for b in range(rows)]
@@ -116,23 +115,6 @@
     for h in range(heads):
         q_s[:, h, :] = rotate(jnp.dot(normed, wq[:, h * dim:(h + 1) * dim], preferred_element_type=F32) + bq[h:h + 1, :].astype(F32))
 
-    @pl.when(middle)
-    def _():
-        each(far[:-1], sent)
-        pl.semaphore_signal(turn, inc=1, device_id={"cp": 3 * layer * high + lax.rem(me, layer) - lax.rem(me, 2)}, device_id_type=MESH)
-
-    @pl.when(end & (lax.rem(me, 2) == 0))
-    def _():
-        pl.semaphore_wait(turn, 2)
-        each(far, start)
-        each(far[:-1], sent)
-        pl.semaphore_signal(turn, inc=1, device_id={"cp": me + 1}, device_id_type=MESH)
-
-    @pl.when(end & second)
-    def _():
-        pl.semaphore_wait(turn, 1)
-        each(far, start)
-
     row = lax.broadcasted_iota(jnp.int32, (m, dim), 0)
     even = lax.rem(row, 2) == 0
 
@@ -186,11 +168,7 @@
     acc[...] = acc[...] / l_s[...]
     att_ref[...] = jnp.concatenate([acc[:, h, :] for h in range(heads)], axis=1).astype(BF16)
 
-    each(beside + near + far[-1:], sent)
-
-    @pl.when(end & second)
-    def _():
-        each(far[:-1], sent)
+    each(beside + near + far, sent)
 
 
 def step(lens, freq, x, gain, b_q, b_k, b_v, w_q, w_k, w_v, w_o, k, v):
@@ -213,7 +191,7 @@
             pltpu.VMEM((rows, heads, dim), F32), pltpu.VMEM((rows, kv, dim), F32), pltpu.VMEM((rows, kv, dim), F32),
             pltpu.VMEM((rows, heads, n * m), F32), pltpu.VMEM((rows, heads, n * m), BF16), pltpu.VMEM((rows, heads, dim), F32),
             pltpu.VMEM((rows, heads, dim), F32),
-            pltpu.SemaphoreType.DMA((2, n)), pltpu.SemaphoreType.DMA((2, n)), pltpu.SemaphoreType.DMA((13,)), pltpu.SemaphoreType.REGULAR],
+            pltpu.SemaphoreType.DMA((2, n)), pltpu.SemaphoreType.DMA((2, n)), pltpu.SemaphoreType.DMA((13,))],
         compiler_params=pltpu.CompilerParams(collective_id=0, has_side_effects=True, vmem_limit_bytes=47 * 1024 * 1024),
     )(lens, freq, x, gain, b_q, b_k, b_v, w_q, w_k, w_v, w_o, k, v)
 

time: 214 us -> 212 us (level)
  no operation moved by 1% of the time
where the time goes in v14:
time: 212 us
  Pallas kernels  212 us (100%)
    pallas_call x1, Pallas kernels, step(): pl.pallas_call(functools.partial(step_kernel, n), out_shape=[pltpu.VMEM(x...  208 us

profile of v14, /device:TPU:29, one launch (start us, length us, event | category | flops | bytes accessed | tf_op | source)
XLA Modules:
  0.0 212.3 jit_solution(9667079776040021891)
XLA Ops:
  0.6 0.0 copy-start
  0.6 207.6 %shard_map.148 = (bf16[8,2048]{1,0:T(8,128)(2,1)S(1)}, bf16[8,16,128,128]{3,2,1,0:T(8,128)(2,1)S(1)}, bf16[8,16,128,128]{3,2,1,0:T(8,128)(2,1)S(1)}, bf16[2048,2048]{1,0:T(8,128)(2,1)S(1)}) custom-call(s32[128]{0:T(128)} %lens_hbm.1, f32[1,128]{1,0:T(1,128)} %constant.2.clone.freq_hbm, bf16[8,2048]{1,0:T(8,128)(2,1)} %x_ref.3, bf16[16,128]{1,0:T(8,128)(2,1)} %bitcast.10, ...), custom_call_target="tpu_custom_call" | custom-call | tf_op jit(solution)/shard_map/pallas_call | solution.py:181
  208.3 0.0 copy-done
  208.3 4.1 %shard_map.149 = (bf16[8,2048]{1,0:T(8,128)(2,1)}, bf16[8,16,128,128]{3,2,1,0:T(8,128)(2,1)}, bf16[8,16,128,128]{3,2,1,0:T(8,128)(2,1)}) custom-call(bf16[8,2048]{1,0:T(8,128)(2,1)S(1)} %copy-done, bf16[8,2048]{1,0:T(8,128)(2,1)S(1)} %get-tuple-element.10.att_ref, bf16[2048,2048]{1,0:T(8,128)(2,1)S(1)} %get-tuple-element.11.wo_ref, ...), custom_call_target="tpu_custom_call" | custom-call | tf_op jit(solution)/shard_map/pallas_call | solution.py:215
Async XLA Ops:
  0.6 207.6 %copy-start = (bf16[8,2048]{1,0:T(8,128)(2,1)S(1)}, bf16[8,2048]{1,0:T(8,128)(2,1)}, u32[]{:S(2)}) copy-start(bf16[8,2048]{1,0:T(8,128)(2,1)} %x_ref.3) | copy-start | bytes 98308

commit v15 on v12

--- a/solution.py
+++ b/solution.py
@@ -66,7 +66,8 @@
     second = lax.rem(me, 2) == 1
     beside = [z * layer + lax.rem(me + t, layer) for t in range(1, layer)]
     near = [(4 * high + 1 - z) * layer + lax.rem(me + t, layer) for t in range(layer)]
-    far = [(1 - high) * half + lax.rem(me + t, half) for t in range(half)]
+    far = [(2 - high) * layer + lax.rem(me + t, layer) for t in range(layer)]
+    far += [3 * (1 - high) * layer + lax.rem(me + t, layer) for t in range(layer)]
 
     def each(targets, act):
         for to in targets:
@@ -79,13 +80,11 @@
     def sent(copy):
         copy.wait_send()
 
-    each(beside, start)
-
     @pl.when(middle)
     def _():
         each(far, start)
 
-    each(near, start)
+    each(near + beside, start)
 
     loads["lens"].wait()
     pos = [lens_ref[me * rows + b] for b in range(rows)]

time: 205 us -> 205 us (level)
  the two profiles are of different devices: /device:TPU:1 before, /device:TPU:0 now
where the time goes in v15:
time: 205 us; the launch traced here: 204 us
  Pallas kernels  203 us (99%)
    pallas_call x1, Pallas kernels, step(): pl.pallas_call(functools.partial(step_kernel, n), out_shape=[pltpu.VMEM(x...  199 us

profile of v15, /device:TPU:0, one launch (start us, length us, event | category | flops | bytes accessed | tf_op | source)
XLA Modules:
  0.0 204.1 jit_solution(3673890066139617806)
XLA Ops:
  0.6 0.0 copy-start
  0.6 199.3 %shard_map.148 = (bf16[8,2048]{1,0:T(8,128)(2,1)S(1)}, bf16[8,16,128,128]{3,2,1,0:T(8,128)(2,1)S(1)}, bf16[8,16,128,128]{3,2,1,0:T(8,128)(2,1)S(1)}, bf16[2048,2048]{1,0:T(8,128)(2,1)S(1)}) custom-call(s32[128]{0:T(128)} %lens_hbm.1, f32[1,128]{1,0:T(1,128)} %constant.2.clone.freq_hbm, bf16[8,2048]{1,0:T(8,128)(2,1)} %x_ref.3, bf16[16,128]{1,0:T(8,128)(2,1)} %bitcast.10, ...), custom_call_target="tpu_custom_call" | custom-call | tf_op jit(solution)/shard_map/pallas_call | solution.py:202
  200.0 0.0 copy-done
  200.0 4.1 %shard_map.149 = (bf16[8,2048]{1,0:T(8,128)(2,1)}, bf16[8,16,128,128]{3,2,1,0:T(8,128)(2,1)}, bf16[8,16,128,128]{3,2,1,0:T(8,128)(2,1)}) custom-call(bf16[8,2048]{1,0:T(8,128)(2,1)S(1)} %copy-done, bf16[8,2048]{1,0:T(8,128)(2,1)S(1)} %get-tuple-element.10.att_ref, bf16[2048,2048]{1,0:T(8,128)(2,1)S(1)} %get-tuple-element.11.wo_ref, ...), custom_call_target="tpu_custom_call" | custom-call | tf_op jit(solution)/shard_map/pallas_call | solution.py:236
Async XLA Ops:
  0.6 199.4 %copy-start = (bf16[8,2048]{1,0:T(8,128)(2,1)S(1)}, bf16[8,2048]{1,0:T(8,128)(2,1)}, u32[]{:S(2)}) copy-start(bf16[8,2048]{1,0:T(8,128)(2,1)} %x_ref.3) | copy-start | bytes 98308

commit v16 on v15

--- a/solution.py
+++ b/solution.py
@@ -80,11 +80,15 @@
     def sent(copy):
         copy.wait_send()
 
-    @pl.when(middle)
+    first = lax.rem(me, 2) == 0
+
+    @pl.when(middle & first)
     def _():
         each(far, start)
 
-    each(near + beside, start)
+    @pl.when(end | second)
+    def _():
+        each(near + beside, start)
 
     loads["lens"].wait()
     pos = [lens_ref[me * rows + b] for b in range(rows)]
@@ -115,22 +119,27 @@
     for h in range(heads):
         q_s[:, h, :] = rotate(jnp.dot(normed, wq[:, h * dim:(h + 1) * dim], preferred_element_type=F32) + bq[h:h + 1, :].astype(F32))
 
-    @pl.when(middle)
-    def _():
+    def hand_over(to):
         each(far[:-1], sent)
-        pl.semaphore_signal(turn, inc=1, device_id={"cp": 3 * layer * high + lax.rem(me, layer) - lax.rem(me, 2)}, device_id_type=MESH)
-
-    @pl.when(end & (lax.rem(me, 2) == 0))
-    def _():
-        pl.semaphore_wait(turn, 2)
-        each(far, start)
-        each(far[:-1], sent)
-        pl.semaphore_signal(turn, inc=1, device_id={"cp": me + 1}, device_id_type=MESH)
-
-    @pl.when(end & second)
+        pl.semaphore_signal(turn, inc=1, device_id={"cp": to}, device_id_type=MESH)
+
+    @pl.when(middle & first)
+    def _():
+        hand_over(me + 1)
+        each(near + beside, start)
+
+    @pl.when(end | second)
     def _():
         pl.semaphore_wait(turn, 1)
         each(far, start)
+
+    @pl.when(middle & second)
+    def _():
+        hand_over(3 * layer * high + lax.rem(me, layer) - 1)
+
+    @pl.when(end & first)
+    def _():
+        hand_over(me + 1)
 
     row = lax.broadcasted_iota(jnp.int32, (m, dim), 0)
     even = lax.rem(row, 2) == 0

time: 205 us -> 213 us (1.039)
  Pallas kernels: 203 us -> 212 us
    pallas_call x1, Pallas kernels: 199 us -> 208 us  [step(): pl.pallas_call(functools.partial(step_kernel, n), out_shape=[pltpu.VMEM(x...]
where the time goes in v16:
time: 213 us; the launch traced here: 212 us
  Pallas kernels  212 us (100%)
    pallas_call x1, Pallas kernels, step(): pl.pallas_call(functools.partial(step_kernel, n), out_shape=[pltpu.VMEM(x...  208 us

profile of v16, /device:TPU:0, one launch (start us, length us, event | category | flops | bytes accessed | tf_op | source)
XLA Modules:
  0.0 212.4 jit_solution(7308492788422160776)
XLA Ops:
  0.6 0.0 copy-start
  0.6 207.6 %shard_map.148 = (bf16[8,2048]{1,0:T(8,128)(2,1)S(1)}, bf16[8,16,128,128]{3,2,1,0:T(8,128)(2,1)S(1)}, bf16[8,16,128,128]{3,2,1,0:T(8,128)(2,1)S(1)}, bf16[2048,2048]{1,0:T(8,128)(2,1)S(1)}) custom-call(s32[128]{0:T(128)} %lens_hbm.1, f32[1,128]{1,0:T(1,128)} %constant.2.clone.freq_hbm, bf16[8,2048]{1,0:T(8,128)(2,1)} %x_ref.3, bf16[16,128]{1,0:T(8,128)(2,1)} %bitcast.10, ...), custom_call_target="tpu_custom_call" | custom-call | tf_op jit(solution)/shard_map/pallas_call | solution.py:211
  208.3 0.0 copy-done
  208.3 4.1 %shard_map.149 = (bf16[8,2048]{1,0:T(8,128)(2,1)}, bf16[8,16,128,128]{3,2,1,0:T(8,128)(2,1)}, bf16[8,16,128,128]{3,2,1,0:T(8,128)(2,1)}) custom-call(bf16[8,2048]{1,0:T(8,128)(2,1)S(1)} %copy-done, bf16[8,2048]{1,0:T(8,128)(2,1)S(1)} %get-tuple-element.10.att_ref, bf16[2048,2048]{1,0:T(8,128)(2,1)S(1)} %get-tuple-element.11.wo_ref, ...), custom_call_target="tpu_custom_call" | custom-call | tf_op jit(solution)/shard_map/pallas_call | solution.py:245
Async XLA Ops:
  0.6 207.7 %copy-start = (bf16[8,2048]{1,0:T(8,128)(2,1)S(1)}, bf16[8,2048]{1,0:T(8,128)(2,1)}, u32[]{:S(2)}) copy-start(bf16[8,2048]{1,0:T(8,128)(2,1)} %x_ref.3) | copy-start | bytes 98308

commit v17 on v15

--- a/solution.py
+++ b/solution.py
@@ -64,10 +64,15 @@
     end = lax.rem(z + high, 2) == 0
     middle = lax.rem(z + high, 2) == 1
     second = lax.rem(me, 2) == 1
-    beside = [z * layer + lax.rem(me + t, layer) for t in range(1, layer)]
-    near = [(4 * high + 1 - z) * layer + lax.rem(me + t, layer) for t in range(layer)]
-    far = [(2 - high) * layer + lax.rem(me + t, layer) for t in range(layer)]
-    far += [3 * (1 - high) * layer + lax.rem(me + t, layer) for t in range(layer)]
+    y, core = lax.rem(lax.div(me, 2), 2), lax.rem(me, 2)
+
+    def chip(z_to, y_to):
+        return [z_to * layer + 2 * y_to + core, z_to * layer + 2 * y_to + 1 - core]
+
+    far_z = (2 - high, 3 * (1 - high))
+    far = [to for y_to in (y, 1 - y) for z_to in far_z for to in chip(z_to, y_to)]
+    near = chip(4 * high + 1 - z, 1 - y) + chip(4 * high + 1 - z, y)
+    beside = chip(z, 1 - y) + chip(z, y)[1:]
 
     def each(targets, act):
         for to in targets:
@@ -84,7 +89,7 @@
     def _():
         each(far, start)
 
-    each(near + beside, start)
+    each(beside + near, start)
 
     loads["lens"].wait()
     pos = [lens_ref[me * rows + b] for b in range(rows)]

time: 205 us -> 197 us (0.961)
  Pallas kernels: 203 us -> 196 us
    pallas_call x1, Pallas kernels: 199 us -> 192 us  [step(): pl.pallas_call(functools.partial(step_kernel, n), out_shape=[pltpu.VMEM(x...]
where the time goes in v17:
time: 197 us; the launch traced here: 196 us
  Pallas kernels  196 us (99%)
    pallas_call x1, Pallas kernels, step(): pl.pallas_call(functools.partial(step_kernel, n), out_shape=[pltpu.VMEM(x...  192 us
    pallas_call x1, Pallas kernels, finish(): pl.pallas_call(finish_kernel, out_shape=[jax.ShapeDtypeStruct(x.shape, BF...  4.07 us

profile of v17, /device:TPU:0, one launch (start us, length us, event | category | flops | bytes accessed | tf_op | source)
XLA Modules:
  0.0 196.5 jit_solution(13559922688700331672)
XLA Ops:
  0.6 0.0 copy-start
  0.6 191.8 %shard_map.148 = (bf16[8,2048]{1,0:T(8,128)(2,1)S(1)}, bf16[8,16,128,128]{3,2,1,0:T(8,128)(2,1)S(1)}, bf16[8,16,128,128]{3,2,1,0:T(8,128)(2,1)S(1)}, bf16[2048,2048]{1,0:T(8,128)(2,1)S(1)}) custom-call(s32[128]{0:T(128)} %lens_hbm.1, f32[1,128]{1,0:T(1,128)} %constant.2.clone.freq_hbm, bf16[8,2048]{1,0:T(8,128)(2,1)} %x_ref.3, bf16[16,128]{1,0:T(8,128)(2,1)} %bitcast.10, ...), custom_call_target="tpu_custom_call" | custom-call | tf_op jit(solution)/shard_map/pallas_call | solution.py:207
  192.4 0.0 copy-done
  192.4 4.1 %shard_map.149 = (bf16[8,2048]{1,0:T(8,128)(2,1)}, bf16[8,16,128,128]{3,2,1,0:T(8,128)(2,1)}, bf16[8,16,128,128]{3,2,1,0:T(8,128)(2,1)}) custom-call(bf16[8,2048]{1,0:T(8,128)(2,1)S(1)} %copy-done, bf16[8,2048]{1,0:T(8,128)(2,1)S(1)} %get-tuple-element.10.att_ref, bf16[2048,2048]{1,0:T(8,128)(2,1)S(1)} %get-tuple-element.11.wo_ref, ...), custom_call_target="tpu_custom_call" | custom-call | tf_op jit(solution)/shard_map/pallas_call | solution.py:241
Async XLA Ops:
  0.6 191.8 %copy-start = (bf16[8,2048]{1,0:T(8,128)(2,1)S(1)}, bf16[8,2048]{1,0:T(8,128)(2,1)}, u32[]{:S(2)}) copy-start(bf16[8,2048]{1,0:T(8,128)(2,1)} %x_ref.3) | copy-start | bytes 98308

commit v18 on v17

--- a/solution.py
+++ b/solution.py
@@ -71,7 +71,7 @@
 
     far_z = (2 - high, 3 * (1 - high))
     far = [to for y_to in (y, 1 - y) for z_to in far_z for to in chip(z_to, y_to)]
-    near = chip(4 * high + 1 - z, 1 - y) + chip(4 * high + 1 - z, y)
+    near = chip(4 * high + 1 - z, y) + chip(4 * high + 1 - z, 1 - y)
     beside = chip(z, 1 - y) + chip(z, y)[1:]
 
     def each(targets, act):
@@ -89,7 +89,11 @@
     def _():
         each(far, start)
 
-    each(beside + near, start)
+    each(beside + near[:2], start)
+
+    @pl.when(end)
+    def _():
+        each(near[2:], start)
 
     loads["lens"].wait()
     pos = [lens_ref[me * rows + b] for b in range(rows)]
@@ -124,6 +128,7 @@
     def _():
         each(far[:-1], sent)
         pl.semaphore_signal(turn, inc=1, device_id={"cp": 3 * layer * high + lax.rem(me, layer) - lax.rem(me, 2)}, device_id_type=MESH)
+        each(near[2:], start)
 
     @pl.when(end & (lax.rem(me, 2) == 0))
     def _():

time: 197 us -> 198 us (level)
  no operation moved by 1% of the time
where the time goes in v18:
time: 198 us; the launch traced here: 197 us
  Pallas kernels  197 us (99%)
    pallas_call x1, Pallas kernels, step(): pl.pallas_call(functools.partial(step_kernel, n), out_shape=[pltpu.VMEM(x...  193 us
    pallas_call x1, Pallas kernels, finish(): pl.pallas_call(finish_kernel, out_shape=[jax.ShapeDtypeStruct(x.shape, BF...  4.07 us

profile of v18, /device:TPU:0, one launch (start us, length us, event | category | flops | bytes accessed | tf_op | source)
XLA Modules:
  0.0 197.5 jit_solution(1489896767105059499)
XLA Ops:
  0.6 0.0 copy-start
  0.6 192.8 %shard_map.148 = (bf16[8,2048]{1,0:T(8,128)(2,1)S(1)}, bf16[8,16,128,128]{3,2,1,0:T(8,128)(2,1)S(1)}, bf16[8,16,128,128]{3,2,1,0:T(8,128)(2,1)S(1)}, bf16[2048,2048]{1,0:T(8,128)(2,1)S(1)}) custom-call(s32[128]{0:T(128)} %lens_hbm.1, f32[1,128]{1,0:T(1,128)} %constant.2.clone.freq_hbm, bf16[8,2048]{1,0:T(8,128)(2,1)} %x_ref.3, bf16[16,128]{1,0:T(8,128)(2,1)} %bitcast.10, ...), custom_call_target="tpu_custom_call" | custom-call | tf_op jit(solution)/shard_map/pallas_call | solution.py:212
  193.4 0.0 copy-done
  193.4 4.1 %shard_map.149 = (bf16[8,2048]{1,0:T(8,128)(2,1)}, bf16[8,16,128,128]{3,2,1,0:T(8,128)(2,1)}, bf16[8,16,128,128]{3,2,1,0:T(8,128)(2,1)}) custom-call(bf16[8,2048]{1,0:T(8,128)(2,1)S(1)} %copy-done, bf16[8,2048]{1,0:T(8,128)(2,1)S(1)} %get-tuple-element.10.att_ref, bf16[2048,2048]{1,0:T(8,128)(2,1)S(1)} %get-tuple-element.11.wo_ref, ...), custom_call_target="tpu_custom_call" | custom-call | tf_op jit(solution)/shard_map/pallas_call | solution.py:246
Async XLA Ops:
  0.6 192.8 %copy-start = (bf16[8,2048]{1,0:T(8,128)(2,1)S(1)}, bf16[8,2048]{1,0:T(8,128)(2,1)}, u32[]{:S(2)}) copy-start(bf16[8,2048]{1,0:T(8,128)(2,1)} %x_ref.3) | copy-start | bytes 98308

commit v19 on v17

--- a/solution.py
+++ b/solution.py
@@ -122,7 +122,7 @@
 
     @pl.when(middle)
     def _():
-        each(far[:-1], sent)
+        each(far[:4], sent)
         pl.semaphore_signal(turn, inc=1, device_id={"cp": 3 * layer * high + lax.rem(me, layer) - lax.rem(me, 2)}, device_id_type=MESH)
 
     @pl.when(end & (lax.rem(me, 2) == 0))
@@ -191,6 +191,10 @@
     att_ref[...] = jnp.concatenate([acc[:, h, :] for h in range(heads)], axis=1).astype(BF16)
 
     each(beside + near + far[-1:], sent)
+
+    @pl.when(middle)
+    def _():
+        each(far[4:-1], sent)
 
     @pl.when(end & second)
     def _():

time: 197 us -> 196 us (level)
  no operation moved by 1% of the time
where the time goes in v19:
time: 196 us
  Pallas kernels  195 us (99%)
    pallas_call x1, Pallas kernels, step(): pl.pallas_call(functools.partial(step_kernel, n), out_shape=[pltpu.VMEM(x...  191 us
    pallas_call x1, Pallas kernels, finish(): pl.pallas_call(finish_kernel, out_shape=[jax.ShapeDtypeStruct(x.shape, BF...  4.07 us

profile of v19, /device:TPU:0, one launch (start us, length us, event | category | flops | bytes accessed | tf_op | source)
XLA Modules:
  0.0 195.6 jit_solution(3905369785462358938)
XLA Ops:
  0.6 0.0 copy-start
  0.6 190.9 %shard_map.148 = (bf16[8,2048]{1,0:T(8,128)(2,1)S(1)}, bf16[8,16,128,128]{3,2,1,0:T(8,128)(2,1)S(1)}, bf16[8,16,128,128]{3,2,1,0:T(8,128)(2,1)S(1)}, bf16[2048,2048]{1,0:T(8,128)(2,1)S(1)}) custom-call(s32[128]{0:T(128)} %lens_hbm.1, f32[1,128]{1,0:T(1,128)} %constant.2.clone.freq_hbm, bf16[8,2048]{1,0:T(8,128)(2,1)} %x_ref.3, bf16[16,128]{1,0:T(8,128)(2,1)} %bitcast.10, ...), custom_call_target="tpu_custom_call" | custom-call | tf_op jit(solution)/shard_map/pallas_call | solution.py:211
  191.5 0.0 copy-done
  191.5 4.1 %shard_map.149 = (bf16[8,2048]{1,0:T(8,128)(2,1)}, bf16[8,16,128,128]{3,2,1,0:T(8,128)(2,1)}, bf16[8,16,128,128]{3,2,1,0:T(8,128)(2,1)}) custom-call(bf16[8,2048]{1,0:T(8,128)(2,1)S(1)} %copy-done, bf16[8,2048]{1,0:T(8,128)(2,1)S(1)} %get-tuple-element.10.att_ref, bf16[2048,2048]{1,0:T(8,128)(2,1)S(1)} %get-tuple-element.11.wo_ref, ...), custom_call_target="tpu_custom_call" | custom-call | tf_op jit(solution)/shard_map/pallas_call | solution.py:245
Async XLA Ops:
  0.6 190.9 %copy-start = (bf16[8,2048]{1,0:T(8,128)(2,1)S(1)}, bf16[8,2048]{1,0:T(8,128)(2,1)}, u32[]{:S(2)}) copy-start(bf16[8,2048]{1,0:T(8,128)(2,1)} %x_ref.3) | copy-start | bytes 98308

commit v20 on v19

--- a/solution.py
+++ b/solution.py
@@ -129,7 +129,7 @@
     def _():
         pl.semaphore_wait(turn, 2)
         each(far, start)
-        each(far[:-1], sent)
+        each(far[:4], sent)
         pl.semaphore_signal(turn, inc=1, device_id={"cp": me + 1}, device_id_type=MESH)
 
     @pl.when(end & second)
@@ -192,7 +192,7 @@
 
     each(beside + near + far[-1:], sent)
 
-    @pl.when(middle)
+    @pl.when(middle | (lax.rem(me, 2) == 0))
     def _():
         each(far[4:-1], sent)
 

time: 196 us -> 196 us (level)
  no operation moved by 1% of the time
where the time goes in v20:
time: 196 us; the launch traced here: 195 us
  Pallas kernels  195 us (99%)
    pallas_call x1, Pallas kernels, step(): pl.pallas_call(functools.partial(step_kernel, n), out_shape=[pltpu.VMEM(x...  191 us
    pallas_call x1, Pallas kernels, finish(): pl.pallas_call(finish_kernel, out_shape=[jax.ShapeDtypeStruct(x.shape, BF...  4.07 us

profile of v20, /device:TPU:0, one launch (start us, length us, event | category | flops | bytes accessed | tf_op | source)
XLA Modules:
  0.0 195.4 jit_solution(13549721520783567245)
XLA Ops:
  0.6 0.0 copy-start
  0.6 190.7 %shard_map.148 = (bf16[8,2048]{1,0:T(8,128)(2,1)S(1)}, bf16[8,16,128,128]{3,2,1,0:T(8,128)(2,1)S(1)}, bf16[8,16,128,128]{3,2,1,0:T(8,128)(2,1)S(1)}, bf16[2048,2048]{1,0:T(8,128)(2,1)S(1)}) custom-call(s32[128]{0:T(128)} %lens_hbm.1, f32[1,128]{1,0:T(1,128)} %constant.2.clone.freq_hbm, bf16[8,2048]{1,0:T(8,128)(2,1)} %x_ref.3, bf16[16,128]{1,0:T(8,128)(2,1)} %bitcast.10, ...), custom_call_target="tpu_custom_call" | custom-call | tf_op jit(solution)/shard_map/pallas_call | solution.py:211
  191.3 0.0 copy-done
  191.3 4.1 %shard_map.149 = (bf16[8,2048]{1,0:T(8,128)(2,1)}, bf16[8,16,128,128]{3,2,1,0:T(8,128)(2,1)}, bf16[8,16,128,128]{3,2,1,0:T(8,128)(2,1)}) custom-call(bf16[8,2048]{1,0:T(8,128)(2,1)S(1)} %copy-done, bf16[8,2048]{1,0:T(8,128)(2,1)S(1)} %get-tuple-element.10.att_ref, bf16[2048,2048]{1,0:T(8,128)(2,1)S(1)} %get-tuple-element.11.wo_ref, ...), custom_call_target="tpu_custom_call" | custom-call | tf_op jit(solution)/shard_map/pallas_call | solution.py:245
Async XLA Ops:
  0.6 190.7 %copy-start = (bf16[8,2048]{1,0:T(8,128)(2,1)S(1)}, bf16[8,2048]{1,0:T(8,128)(2,1)}, u32[]{:S(2)}) copy-start(bf16[8,2048]{1,0:T(8,128)(2,1)} %x_ref.3) | copy-start | bytes 98308

commit v21 on v14

--- a/solution.py
+++ b/solution.py
@@ -63,9 +63,15 @@
     high = lax.div(me, half)
     end = lax.rem(z + high, 2) == 0
     middle = lax.rem(z + high, 2) == 1
-    beside = [z * layer + lax.rem(me + t, layer) for t in range(1, layer)]
-    near = [(4 * high + 1 - z) * layer + t for t in range(layer)]
-    far = [(1 - high) * half + t for t in range(half)]
+    y, core = lax.rem(lax.div(me, 2), 2), lax.rem(me, 2)
+
+    def chip(z_to, y_to):
+        return [z_to * layer + 2 * y_to + core, z_to * layer + 2 * y_to + 1 - core]
+
+    far_z = (2 - high, 3 * (1 - high))
+    far = [to for y_to in (y, 1 - y) for z_to in far_z for to in chip(z_to, y_to)]
+    near = chip(4 * high + 1 - z, y) + chip(4 * high + 1 - z, 1 - y)
+    beside = chip(z, 1 - y) + chip(z, y)[1:]
 
     def each(targets, act):
         for to in targets:
@@ -80,7 +86,7 @@
 
     @pl.when(middle)
     def _():
-        each(far[:6] + beside + near + far[6:], start)
+        each(beside + far + near, start)
 
     @pl.when(end)
     def _():

time: 212 us -> 196 us (0.925)
  the two profiles are of different devices: /device:TPU:29 before, /device:TPU:0 now
where the time goes in v21:
time: 196 us; the launch traced here: 195 us
  Pallas kernels  195 us (99%)
    pallas_call x1, Pallas kernels, step(): pl.pallas_call(functools.partial(step_kernel, n), out_shape=[pltpu.VMEM(x...  191 us
    pallas_call x1, Pallas kernels, finish(): pl.pallas_call(finish_kernel, out_shape=[jax.ShapeDtypeStruct(x.shape, BF...  4.07 us

profile of v21, /device:TPU:0, one launch (start us, length us, event | category | flops | bytes accessed | tf_op | source)
XLA Modules:
  0.0 195.5 jit_solution(16235442311511120494)
XLA Ops:
  0.6 0.0 copy-start
  0.6 190.8 %shard_map.148 = (bf16[8,2048]{1,0:T(8,128)(2,1)S(1)}, bf16[8,16,128,128]{3,2,1,0:T(8,128)(2,1)S(1)}, bf16[8,16,128,128]{3,2,1,0:T(8,128)(2,1)S(1)}, bf16[2048,2048]{1,0:T(8,128)(2,1)S(1)}) custom-call(s32[128]{0:T(128)} %lens_hbm.1, f32[1,128]{1,0:T(1,128)} %constant.2.clone.freq_hbm, bf16[8,2048]{1,0:T(8,128)(2,1)} %x_ref.3, bf16[16,128]{1,0:T(8,128)(2,1)} %bitcast.10, ...), custom_call_target="tpu_custom_call" | custom-call | tf_op jit(solution)/shard_map/pallas_call | solution.py:187
  191.4 0.0 copy-done
  191.4 4.1 %shard_map.149 = (bf16[8,2048]{1,0:T(8,128)(2,1)}, bf16[8,16,128,128]{3,2,1,0:T(8,128)(2,1)}, bf16[8,16,128,128]{3,2,1,0:T(8,128)(2,1)}) custom-call(bf16[8,2048]{1,0:T(8,128)(2,1)S(1)} %copy-done, bf16[8,2048]{1,0:T(8,128)(2,1)S(1)} %get-tuple-element.10.att_ref, bf16[2048,2048]{1,0:T(8,128)(2,1)S(1)} %get-tuple-element.11.wo_ref, ...), custom_call_target="tpu_custom_call" | custom-call | tf_op jit(solution)/shard_map/pallas_call | solution.py:221
Async XLA Ops:
  0.6 190.8 %copy-start = (bf16[8,2048]{1,0:T(8,128)(2,1)S(1)}, bf16[8,2048]{1,0:T(8,128)(2,1)}, u32[]{:S(2)}) copy-start(bf16[8,2048]{1,0:T(8,128)(2,1)} %x_ref.3) | copy-start | bytes 98308
